TPU v7x, 8 devices: a whole 2x2x1 slice. The times are simulated.
8 devices in a mesh: replica: 1 (over z), data2: 2 (over y), data: 4 (over x, core).
Axes of the slice: x: 2, y: 2, z: 1, core: 2. Of those that a mesh axis runs over, the one named last changes fastest.
Arguments:
- query_hidden: bfloat16 [128, 32, 1536], P(('replica', 'data2', 'data'))
- doc_hidden: bfloat16 [128, 768, 1536], P(('replica', 'data2', 'data'))
- w_proj: bfloat16 [1536, 128], replicated
- query_mask: int32 [128, 32], P(('replica', 'data2', 'data'))
- doc_mask: int32 [128, 768], P(('replica', 'data2', 'data'))
- temperature: float32 [], replicated
Outputs:
- output 1: float32 [128], P(('replica', 'data2', 'data'))
- output 2: float32 [1], P('replica')
All inputs are finite; a program needn't handle non-finite values.
Results may differ from a plain program's by a relative error of at most 0.001.
Values are sent between devices in bfloat16 or wider.
A program may use at most 1 GiB of HBM per device.

v0:
```python
import jax
import jax.numpy as jnp
from jax import lax
from jax.sharding import PartitionSpec as P


def project_norm(hidden, w_proj):
    projected = jnp.einsum('bld,de->ble', hidden, w_proj, preferred_element_type=jnp.float32)
    norm_len = jnp.sqrt(jnp.sum(projected * projected, axis=-1, keepdims=True))
    return (projected / jnp.maximum(norm_len, 1e-12)).astype(jnp.bfloat16)


def tile_scores(q_block, p_block, doc_valid):
    similarity = jnp.einsum('qtc,jsc->qtjs', q_block, p_block, preferred_element_type=jnp.float32)
    best_match = jnp.max(jnp.where(doc_valid[None, None], similarity, -jnp.inf), axis=-1)
    return jnp.sum(best_match, axis=1)


def solution(mesh):
    outer_size = mesh.shape['data2']
    inner_size = mesh.shape['data']
    group_size = outer_size * inner_size
    batch_axes = ('data2', 'data')
    row_spec = P(('replica', 'data2', 'data'))
    tok_spec = P(('replica', 'data2', 'data'), None, None)
    mask_spec = P(('replica', 'data2', 'data'), None)

    def local_step(query_hidden, doc_hidden, w_proj, query_mask, doc_mask, value_a11):
        local_batch = query_hidden.shape[0]
        total_batch = local_batch * group_size
        q_vecs = project_norm(query_hidden, w_proj)
        q_vecs = jnp.where(query_mask[:, :, None] > 0, q_vecs, jnp.zeros_like(q_vecs))
        p_vecs = project_norm(doc_hidden, w_proj)
        doc_valid = doc_mask > 0
        q_all = lax.all_gather(q_vecs, 'data', axis=0, tiled=True)
        q_all = lax.all_gather(q_all, 'data2', axis=0, tiled=True)
        q_blocks = q_all.reshape(group_size, local_batch, q_all.shape[1], q_all.shape[2])
        column = lax.map(lambda q_block: tile_scores(q_block, p_vecs, doc_valid), q_blocks)
        column = column.reshape(outer_size, inner_size, local_batch, local_batch)
        column = lax.all_to_all(column, 'data', 1, 1, tiled=True)
        column = lax.all_to_all(column, 'data2', 0, 0, tiled=True)
        score_row = jnp.transpose(column, (2, 0, 1, 3)).reshape(local_batch, total_batch)
        logits = score_row / value_a11
        home_index = lax.axis_index('data2') * inner_size + lax.axis_index('data')
        own_logits = lax.dynamic_slice_in_dim(logits, home_index * local_batch, local_batch, axis=1)
        losses = jax.nn.logsumexp(logits, axis=1) - jnp.diagonal(own_logits)
        mean_loss = lax.psum(jnp.sum(losses), batch_axes) / total_batch
        return losses, mean_loss.reshape(1)

    return jax.shard_map(local_step, mesh=mesh, in_specs=(tok_spec, tok_spec, P(None, None), mask_spec, mask_spec, P()), out_specs=(row_spec, P('replica')), check_vma=False)
```

profile of v0, /device:TPU:0, one launch (start us, length us, event | category | flops | bytes accessed | tf_op | source)
XLA Modules:
  0.0 147.8 jit_solution(15270891234094373361)
XLA Ops:
  7.2 1.4 copy-done
  8.6 1.6 %multiply_reduce_fusion.1 = (f32[16,32]{1,0:T(8,128)S(1)}, f32[16,32,128]{2,1,0:T(8,128)S(1)}) fusion(bf16[16,32,1536]{2,1,0:T(8,128)(2,1)S(1)} %copy-done, bf16[1536,128]{1,0:T(8,128)(2,1)} %param.10), kind=kOutput, calls=%fused_computation.14 | convolution fusion | flops 201457152 | bytes 2230272 | tf_op jit(solution)/shard_map/bld,de->ble/dot_general | solution.py:8
  10.2 0.7 broadcast_compare_fusion.1
  10.9 0.2 fusion.8
  11.2 11.9 %all_gather.6 = bf16[64,32,128]{2,1,0:T(8,128)(2,1)} all-gather(bf16[16,32,128]{2,1,0:T(8,128)(2,1)S(1)} %fusion.8), channel_id=1, replica_groups=mesh['replica'=1,'data2'=2,'data'=4] {'data'}, dimensions={0}, use_global_device_ids=true | all-gather | bytes 655360 | tf_op jit(solution)/shard_map/all_gather | solution.py:35
  23.0 20.2 %multiply_reduce_fusion = (f32[16,768]{1,0:T(8,128)S(1)}, f32[16,768,128]{1,2,0:T(8,128)}) fusion(bf16[16,768,1536]{2,1,0:T(8,128)(2,1)} %param.9, bf16[1536,128]{1,0:T(8,128)(2,1)} %param.10), kind=kOutput, calls=%fused_computation.8 | convolution fusion | flops 4834971648 | bytes 44482560 | tf_op jit(solution)/shard_map/bld,de->ble/dot_general | solution.py:8
  43.3 5.1 %divide_convert_fusion = bf16[16,768,128]{1,2,0:T(8,128)(2,1)} fusion(f32[16,768,128]{1,2,0:T(8,128)} %get-tuple-element.67, f32[16,768]{1,0:T(8,128)S(1)} %sqrt_maximum_fusion), kind=kLoop, calls=%fused_computation.7 | loop fusion | flops 3145728 | bytes 9486336 | tf_op jit(solution)/shard_map/convert_element_type | solution.py:10
  48.4 4.6 %copy.18 = bf16[16,768,128]{2,1,0:T(8,128)(2,1)} copy(bf16[16,768,128]{1,2,0:T(8,128)(2,1)} %divide_convert_fusion) | data formatting | bytes 6291456 | tf_op jit(solution)/shard_map/while | solution.py:38
  53.1 45.2 %while.10 = (s32[]{:T(128)}, f32[8,16,16]{2,1,0:T(8,128)S(1)}, pred[16,768]{1,0:T(8,128)(4,1)S(1)}, bf16[8,16,32,128]{3,2,1,0:T(8,128)(2,1)}, bf16[16,768,128]{2,1,0:T(8,128)(2,1)}, /*index=5*/s32[]{:T(128)}, f32[]{:T(128)}) while((s32[]{:T(128)}, f32[8,16,16]{2,1,0:T(8,128)S(1)}, pred[16,768]{1,0:T(8,128)(4,1)S(1)}, ...), condition=%wide.region_5.6_spmd, body=%wide.region_2.5_spmd.sunk | while | flops 1623195392 | bytes 3372629 | solution.py:38
  53.1 5.5 %select_reduce_fusion.2 = f32[16,32,16]{1,2,0:T(8,128)S(1)} fusion(pred[16,768]{1,0:T(8,128)(4,1)S(1)} %get-tuple-element.115, bf16[16,768,128]{2,1,0:T(8,128)(2,1)} %get-tuple-element.117, bf16[8,16,32,128]{3,2,1,0:T(8,128)(2,1)} %get-tuple-element.116, s32[]{:T(128)} %get-tuple-element.106), kind=kOutput, calls=%fused_computation.1.clone.1 | convolution fusion | flops 1623187456 | bytes 3322368 | tf_op jit(solution)/shard_map/while/body/eval_jaxpr/qtc,jsc->qtjs/dot_general | solution.py:14
  58.7 5.5 %select_reduce_fusion.2 = f32[16,32,16]{1,2,0:T(8,128)S(1)} fusion(pred[16,768]{1,0:T(8,128)(4,1)S(1)} %get-tuple-element.115, bf16[16,768,128]{2,1,0:T(8,128)(2,1)} %get-tuple-element.117, bf16[8,16,32,128]{3,2,1,0:T(8,128)(2,1)} %get-tuple-element.116, s32[]{:T(128)} %get-tuple-element.106), kind=kOutput, calls=%fused_computation.1.clone.1 | convolution fusion | flops 1623187456 | bytes 3322368 | tf_op jit(solution)/shard_map/while/body/eval_jaxpr/qtc,jsc->qtjs/dot_general | solution.py:14
  64.4 5.5 %select_reduce_fusion.2 = f32[16,32,16]{1,2,0:T(8,128)S(1)} fusion(pred[16,768]{1,0:T(8,128)(4,1)S(1)} %get-tuple-element.115, bf16[16,768,128]{2,1,0:T(8,128)(2,1)} %get-tuple-element.117, bf16[8,16,32,128]{3,2,1,0:T(8,128)(2,1)} %get-tuple-element.116, s32[]{:T(128)} %get-tuple-element.106), kind=kOutput, calls=%fused_computation.1.clone.1 | convolution fusion | flops 1623187456 | bytes 3322368 | tf_op jit(solution)/shard_map/while/body/eval_jaxpr/qtc,jsc->qtjs/dot_general | solution.py:14
  70.0 5.5 %select_reduce_fusion.2 = f32[16,32,16]{1,2,0:T(8,128)S(1)} fusion(pred[16,768]{1,0:T(8,128)(4,1)S(1)} %get-tuple-element.115, bf16[16,768,128]{2,1,0:T(8,128)(2,1)} %get-tuple-element.117, bf16[8,16,32,128]{3,2,1,0:T(8,128)(2,1)} %get-tuple-element.116, s32[]{:T(128)} %get-tuple-element.106), kind=kOutput, calls=%fused_computation.1.clone.1 | convolution fusion | flops 1623187456 | bytes 3322368 | tf_op jit(solution)/shard_map/while/body/eval_jaxpr/qtc,jsc->qtjs/dot_general | solution.py:14
  75.7 5.5 %select_reduce_fusion.2 = f32[16,32,16]{1,2,0:T(8,128)S(1)} fusion(pred[16,768]{1,0:T(8,128)(4,1)S(1)} %get-tuple-element.115, bf16[16,768,128]{2,1,0:T(8,128)(2,1)} %get-tuple-element.117, bf16[8,16,32,128]{3,2,1,0:T(8,128)(2,1)} %get-tuple-element.116, s32[]{:T(128)} %get-tuple-element.106), kind=kOutput, calls=%fused_computation.1.clone.1 | convolution fusion | flops 1623187456 | bytes 3322368 | tf_op jit(solution)/shard_map/while/body/eval_jaxpr/qtc,jsc->qtjs/dot_general | solution.py:14
  81.3 5.5 %select_reduce_fusion.2 = f32[16,32,16]{1,2,0:T(8,128)S(1)} fusion(pred[16,768]{1,0:T(8,128)(4,1)S(1)} %get-tuple-element.115, bf16[16,768,128]{2,1,0:T(8,128)(2,1)} %get-tuple-element.117, bf16[8,16,32,128]{3,2,1,0:T(8,128)(2,1)} %get-tuple-element.116, s32[]{:T(128)} %get-tuple-element.106), kind=kOutput, calls=%fused_computation.1.clone.1 | convolution fusion | flops 1623187456 | bytes 3322368 | tf_op jit(solution)/shard_map/while/body/eval_jaxpr/qtc,jsc->qtjs/dot_general | solution.py:14
  87.0 5.5 %select_reduce_fusion.2 = f32[16,32,16]{1,2,0:T(8,128)S(1)} fusion(pred[16,768]{1,0:T(8,128)(4,1)S(1)} %get-tuple-element.115, bf16[16,768,128]{2,1,0:T(8,128)(2,1)} %get-tuple-element.117, bf16[8,16,32,128]{3,2,1,0:T(8,128)(2,1)} %get-tuple-element.116, s32[]{:T(128)} %get-tuple-element.106), kind=kOutput, calls=%fused_computation.1.clone.1 | convolution fusion | flops 1623187456 | bytes 3322368 | tf_op jit(solution)/shard_map/while/body/eval_jaxpr/qtc,jsc->qtjs/dot_general | solution.py:14
  92.6 5.5 %select_reduce_fusion.2 = f32[16,32,16]{1,2,0:T(8,128)S(1)} fusion(pred[16,768]{1,0:T(8,128)(4,1)S(1)} %get-tuple-element.115, bf16[16,768,128]{2,1,0:T(8,128)(2,1)} %get-tuple-element.117, bf16[8,16,32,128]{3,2,1,0:T(8,128)(2,1)} %get-tuple-element.116, s32[]{:T(128)} %get-tuple-element.106), kind=kOutput, calls=%fused_computation.1.clone.1 | convolution fusion | flops 1623187456 | bytes 3322368 | tf_op jit(solution)/shard_map/while/body/eval_jaxpr/qtc,jsc->qtjs/dot_general | solution.py:14
  98.3 0.1 reshape.53
  98.4 6.2 %all_to_all.10 = f32[4,1,512]{2,1,0:T(1,128)S(1)} all-to-all(f32[4,1,512]{2,1,0:T(1,128)S(1)} %reshape.53), channel_id=1, replica_groups=mesh['replica'=1,'data2'=2,'data'=4] {'data'}, dimensions={0} | all-to-all | bytes 16384 | tf_op jit(solution)/shard_map/all_to_all | solution.py:40
  104.6 0.5 broadcast.60
  105.1 0.7 reduce.4
  105.8 0.1 reshape.54
  106.0 0.7 reshape.55
  106.7 3.2 %all-to-all-start.1 = ((f32[2,1,1024]{2,1,0:T(1,128)}), f32[2,1,1024]{2,1,0:T(1,128)S(1)}, u32[]{:S(2)}, u32[]{:S(2)}) async-start(f32[2,1,1024]{2,1,0:T(1,128)} %reshape.55), calls=%async_computation.1 | async-start | bytes 16384 | tf_op jit(solution)/shard_map/all_to_all | solution.py:41
  110.6 2.9 %all-to-all-done.1 = f32[2,1,1024]{2,1,0:T(1,128)S(1)} async-done(((f32[2,1,1024]{2,1,0:T(1,128)}), f32[2,1,1024]{2,1,0:T(1,128)S(1)}, u32[]{:S(2)}, u32[]{:S(2)}) %all-to-all-start.1) | async-done | bytes 8224 | tf_op jit(solution)/shard_map/all_to_all | solution.py:41
  113.5 0.7 reduce.5
  114.2 0.1 reshape.56
  114.3 0.2 fusion.10
  114.6 0.3 exponential_reduce_fusion
  115.0 0.7 gather_fusion
  115.7 1.1 fusion.9
  116.8 22.4 %psum.7 = f32[]{:T(128)} all-reduce(f32[]{:T(128)} %get-tuple-element.60), channel_id=1, replica_groups=mesh['replica'=1,'data2'=2,'data'=4] {'data2','data'}, use_global_device_ids=true, to_apply=%region_9.10 | all-reduce | flops 1 | bytes 8 | tf_op jit(solution)/shard_map/psum | solution.py:47
  (33 shorter events, 1.3 us)
Async XLA Ops:
  7.2 1.4 copy-start
  7.2 45.9 %all-gather.2.cloned.1.call-start = ((), (), s32[]{:S(2)}) async-start(), calls=%async_computation.2 | async-start | bytes 1572864 | tf_op jit(solution)/shard_map/all_gather | solution.py:36
  43.3 9.8 %copy-start.1 = (s32[16,768]{1,0:T(8,128)S(1)}, s32[16,768]{1,0:T(8,128)}, u32[]{:S(2)}) copy-start(s32[16,768]{1,0:T(8,128)} %param.12) | copy-start | bytes 147460
  106.7 6.8 %all-to-all-start.1 = ((f32[2,1,1024]{2,1,0:T(1,128)}), f32[2,1,1024]{2,1,0:T(1,128)S(1)}, u32[]{:S(2)}, u32[]{:S(2)}) async-start(f32[2,1,1024]{2,1,0:T(1,128)} %reshape.55), calls=%async_computation.1 | async-start | bytes 16384 | tf_op jit(solution)/shard_map/all_to_all | solution.py:41
Sparse Core Ops, SparseCore 0:
  23.2 18.3 all-gather.1
where the time goes:
time: 149 us; the launch traced here: 148 us
  matrix products  65.8 us (44%)
  blocking collectives  40.4 us (27%)
  between operations  16.6 us (11%)
  other arithmetic  9.91 us (7%)
  local copies, waits for them, and re-layouts  8.62 us (6%)
  starting transfers between devices  3.26 us (2%)
  waiting for transfers between devices  2.96 us (2%)
    dot_general x8, matrix products, tile_scores(): jnp.einsum('qtc,jsc->qtjs', q_block, p_block, preferred_element_type=jnp....  43.9 us
    psum x1, blocking collectives, local_step(): mean_loss = lax.psum(jnp.sum(losses), batch_axes) / total_batch  22.4 us
    dot_general x2, matrix products, project_norm(): jnp.einsum('bld,de->ble', hidden, w_proj, preferred_element_type=jnp.floa...  21.8 us
    all_gather x1, blocking collectives, local_step(): q_all = lax.all_gather(q_vecs, 'data', axis=0, tiled=True)  11.9 us
    all_to_all x1, blocking collectives, local_step(): column = lax.all_to_all(column, 'data', 1, 1, tiled=True)  6.15 us
    convert_element_type x1, other arithmetic, project_norm(): return (projected / jnp.maximum(norm_len, 1e-12)).astype(jnp.bfloat16)  5.11 us
    while x1, local copies, waits for them, and re-layouts, local_step(): lax.map(lambda q_block: tile_scores(q_block, p_vecs, doc_valid), q_blocks)  4.64 us
    all_to_all x1, starting transfers between devices, local_step(): column = lax.all_to_all(column, 'data2', 0, 0, tiled=True)  3.22 us
  transfers between devices with their start and end apart: 2, of which 1 were waited for; matrix products, arithmetic and copies ran while one was open for 20% of the time, Pallas kernels for 0%

commit v1 on v0

v1 whole, which is shorter than its diff:
```python
import functools

import jax
import jax.numpy as jnp
from jax import lax
from jax.experimental import pallas as pl
from jax.experimental.pallas import tpu as pltpu
from jax.sharding import PartitionSpec as P

MESH = pl.DeviceIdType.MESH
F32, BF16 = jnp.float32, jnp.bfloat16
BIG = 1e30
UNIT = 64
LANES = 8
RING = 6


def iota(shape, dim):
    return lax.broadcasted_iota(jnp.int32, shape, dim)


def dot(a, b):
    return jnp.dot(a, b, preferred_element_type=F32)


def place(rel):
    y, d = lax.axis_index('data2'), lax.axis_index('data')
    x, core = d // 2, d % 2
    y = 1 - y if rel & 4 else y
    x = 1 - x if rel & 2 else x
    core = 1 - core if rel & 1 else core
    return {'data2': y, 'data': x * 2 + core}, y * 4 + x * 2 + core


def unit_rows(projected):
    square = jnp.sum(projected * projected, axis=-1, keepdims=True)
    return (projected * lax.rsqrt(jnp.maximum(square, 1e-24))).astype(BF16)


def project_kernel(nq, qlen, nd, dlen, q_hbm, d_hbm, w_hbm, qm_hbm, dm_hbm, q_all, qm_all, p_ext, table,
                   q_buf, w_buf, dm_buf, nmt, d_buf, in_sem, d_sem, qs_sem, qr_sem, ms_sem, mr_sem):
    rows = nq * qlen
    me = place(0)[1]
    my_mask = qm_all.at[pl.ds(me * nq, nq)]
    ins = [pltpu.make_async_copy(src, dst, in_sem.at[k]) for k, (src, dst) in enumerate(
        [(qm_hbm, my_mask), (dm_hbm, dm_buf), (w_hbm, w_buf), (q_hbm, q_buf)])]
    for copy in ins:
        copy.start()

    def doc_copy(j, slot):
        return pltpu.make_async_copy(d_hbm.at[pl.ds(j * dlen, dlen)], d_buf.at[slot], d_sem.at[slot])

    for j in range(RING):
        doc_copy(j, j).start()

    barrier = pltpu.get_barrier_semaphore()
    for rel in (1, 2, 4, 6):
        pl.semaphore_signal(barrier, inc=1, device_id=place(rel)[0], device_id_type=MESH)

    ins[0].wait()
    mask = qm_all[pl.ds(me * nq, nq), :].astype(F32).astype(BF16)
    spread = dot(mask, (iota((qlen, rows), 1) % qlen == iota((qlen, rows), 0)).astype(F32).astype(BF16))
    flat = jnp.sum(jnp.where(iota((nq, rows), 1) // qlen == iota((nq, rows), 0), spread, 0.0), axis=0, keepdims=True)
    before = (iota((rows, rows), 0) < iota((rows, rows), 1)).astype(F32).astype(BF16)
    rank = dot(jnp.broadcast_to(flat, (16, rows)).astype(BF16), before)[0:1]
    rank = jnp.where(flat > 0.5, rank, -1.0).astype(jnp.int32)
    pick = (iota((rows, rows), 0) == rank).astype(F32).astype(BF16)

    ins[1].wait()
    dmask = dm_buf[...]
    off = jnp.concatenate([1.0 - dmask.astype(F32), jnp.zeros((128 - nd, dlen), F32)], axis=0)
    nmt[...] = jnp.transpose(off).astype(BF16)
    last = jnp.max(dmask * (iota((nd, dlen), 1) + 1), axis=1, keepdims=True).astype(F32)
    per_doc = dlen // UNIT
    count = jnp.floor((last + (UNIT - 1.0)) * (1.0 / UNIT))
    wide = jnp.broadcast_to(count, (nd, 128))
    upto = dot((iota((nd, nd), 0) >= iota((nd, nd), 1)).astype(F32).astype(BF16), wide.astype(BF16))[:, 0:1]
    total = jnp.max(upto, axis=0, keepdims=True)
    slot_id = jnp.minimum(iota((nd, 256), 1).astype(F32), total - 1.0)
    passed = slot_id >= upto
    unit = slot_id[0:1] + jnp.sum(jnp.where(passed, per_doc - count, 0.0), axis=0, keepdims=True)
    doc = jnp.sum(jnp.where(passed, 1.0, 0.0), axis=0, keepdims=True)
    table[0:1, :] = unit.astype(jnp.int32)
    table[1:2, :] = doc.astype(jnp.int32)
    table[2:3, :] = jnp.broadcast_to(total, (1, 256)).astype(jnp.int32)

    ins[2].wait()
    ins[3].wait()
    q_vec = unit_rows(dot(q_buf[...], w_buf[...]))
    q_all[pl.ds(me * rows, rows), :] = dot(pick, q_vec).astype(BF16)
    pl.semaphore_wait(barrier, 4)

    def send(origin_rel, to_rel, k):
        origin = place(origin_rel)[1]
        arrive = origin_rel ^ to_rel
        target = place(to_rel)[0]
        q_ref, m_ref = q_all.at[pl.ds(origin * rows, rows)], qm_all.at[pl.ds(origin * nq, nq)]
        pair = [pltpu.make_async_remote_copy(src_ref=ref, dst_ref=ref, send_sem=ss.at[k], recv_sem=rs.at[arrive - 1],
                                             device_id=target, device_id_type=MESH)
                for ref, ss, rs in ((m_ref, ms_sem, mr_sem), (q_ref, qs_sem, qr_sem))]
        for copy in pair:
            copy.start()
        return pair

    def received(rel):
        origin = place(rel)[1]
        q_ref, m_ref = q_all.at[pl.ds(origin * rows, rows)], qm_all.at[pl.ds(origin * nq, nq)]
        for ref, ss, rs in ((m_ref, ms_sem, mr_sem), (q_ref, qs_sem, qr_sem)):
            pltpu.make_async_remote_copy(src_ref=ref, dst_ref=ref, send_sem=ss.at[0], recv_sem=rs.at[rel - 1],
                                         device_id=place(rel)[0], device_id_type=MESH).wait_recv()

    sent = [send(0, rel, k) for k, rel in enumerate((2, 4, 6, 1))]

    def project(j, carry):
        slot = lax.rem(j, RING)
        doc_copy(j, slot).wait()
        p_ext[pl.ds(j * dlen, dlen), 0:128] = unit_rows(dot(d_buf[slot], w_buf[...]))
        p_ext[pl.ds(j * dlen, dlen), 128:256] = jnp.where(iota((dlen, 128), 1) == j, nmt[...].astype(F32), 0.0).astype(BF16)

        @pl.when(j + RING < nd)
        def _():
            doc_copy(j + RING, slot).start()

        return carry

    split = (5 * nd) // 8
    lax.fori_loop(0, split, project, 0)
    for k, rel in enumerate((2, 4)):
        received(rel)
        sent.append(send(rel, 1, 4 + k))
    lax.fori_loop(split, nd, project, 0)
    received(6)
    sent.append(send(6, 1, 6))
    for rel in (1, 3, 5, 7):
        received(rel)

    lane = iota((1, 256), 1)
    start = jnp.zeros((1, 1), jnp.int32)
    starts = jnp.zeros((1, 256), jnp.int32)
    for dev in range(8):
        starts = starts + jnp.where(lane == dev, start, 0)
        valid = jnp.sum(jnp.sum(qm_all[dev * nq:(dev + 1) * nq, :].astype(F32), axis=1, keepdims=True), axis=0, keepdims=True)
        start = start + (jnp.floor((valid + 15.0) * (1.0 / 16.0)) * 16.0).astype(jnp.int32)
    table[3:4, :] = starts + jnp.where(lane == 8, start, 0)
    for pair in sent:
        for copy in pair:
            copy.wait_send()


def score_body(nd, rows, tiles, table, q_all, p_ext, out, q_list, best, accs):
    floor = jnp.full((nd, 8, 256), -3e38, F32)
    out[...] = jnp.zeros_like(out)
    for dev in range(8):
        q_list[pl.ds(pl.multiple_of(table[3, dev], 16), rows), :] = q_all[dev * rows:(dev + 1) * rows, :]
    q_list[pl.ds(pl.multiple_of(table[3, 7], 16) + rows, 256), :] = jnp.zeros((256, 128), BF16)
    n_tile = (table[3, 8] + 255) // 256
    n_trip = (table[2, 0] + (2 * LANES - 1)) // (2 * LANES)
    away = jnp.full((256, 128), -BIG, BF16)

    def push(tile):
        q_tile = q_list[pl.ds(pl.multiple_of(tile * 256, 256), 256), :]
        rhs = jnp.concatenate([q_tile, away], axis=1)
        for unit in range(2):
            pltpu.matmul_push_rhs(rhs, staging_register=0, mxu_index=unit, transpose=True)

    def drain(unit, k, slot, trip):
        value = pltpu.matmul_pop(accs[unit][k])
        top = value[0:8]
        for r in range(1, UNIT // 8):
            top = jnp.maximum(top, value[8 * r:8 * r + 8])
        doc = table[1, trip * (2 * LANES) + 2 * k + unit]
        best[unit][slot, doc] = jnp.maximum(best[unit][slot, doc], top)

    def step(slot, trip, prev_slot, prev_trip, first):
        for k in range(LANES):
            for unit in range(2):
                drain(unit, k, prev_slot, prev_trip)
                row = table[0, trip * (2 * LANES) + 2 * k + unit] * UNIT
                lhs = p_ext[pl.ds(pl.multiple_of(row, UNIT), UNIT), :]
                pltpu.matmul_acc_lhs(accs[unit][k], lhs, load_staged_rhs=0 if first and k == 0 else None)

    def finish(slot, tile):
        both = jnp.maximum(best[0][slot], best[1][slot])
        out[tile] = jnp.max(both, axis=1)

    for unit in range(2):
        for k in range(LANES):
            pltpu.matmul_pop(accs[unit][k])
    push(0)

    def per_tile(tile, carry):
        best[0][tile + 1] = floor
        best[1][tile + 1] = floor
        step(tile + 1, 0, tile, n_trip - 1, True)
        finish(tile, jnp.maximum(tile - 1, 0))
        push(jnp.minimum(tile + 1, tiles - 1))

        def per_trip(trip, carry):
            step(tile + 1, trip, tile + 1, trip - 1, False)
            return carry

        lax.fori_loop(1, n_trip, per_trip, 0)
        return carry

    best[0][0] = floor
    best[1][0] = floor
    lax.fori_loop(0, n_tile, per_tile, 0)
    for k in range(LANES):
        for unit in range(2):
            drain(unit, k, n_tile, n_trip - 1)
    finish(n_tile, n_tile - 1)
    for unit in range(2):
        pltpu.matmul_acc_lhs(accs[unit][0], jnp.zeros((UNIT, 256), BF16), load_staged_rhs=0)
        pltpu.matmul_pop(accs[unit][0])


def score_kernel(nd, rows, tiles, table, q_all, p_ext, out, q_list, best0, best1):
    def body(*accs):
        score_body(nd, rows, tiles, table, q_all, p_ext, out, q_list, (best0, best1), (accs[:LANES], accs[LANES:]))

    pl.run_scoped(body, *[pltpu.ACC(0)((UNIT, 256), F32)] * LANES, *[pltpu.ACC(1)((UNIT, 256), F32)] * LANES)


def loss_kernel(nq, nd, qlen, tiles, temp, best, qm_all, losses, mean, seg, scores, send_sem, recv_sem):
    n = nq * 8
    me = place(0)[1]
    barrier = pltpu.get_barrier_semaphore()
    for rel in range(1, 8):
        pl.semaphore_signal(barrier, inc=1, device_id=place(rel)[0], device_id_type=MESH)

    col = iota((n, n), 1)
    row = iota((n, n), 0)
    as_bf = lambda cond: cond.astype(F32).astype(BF16)
    mask = qm_all[...].astype(F32).astype(BF16)
    counts = lax.dot_general(jnp.ones((16, qlen), BF16), mask, (((1,), (1,)), ((), ())), preferred_element_type=F32)
    counts_bf = counts.astype(BF16)
    in_dev = dot(counts_bf, as_bf((row // nq == col // nq) & (row < col)))
    valid = dot(counts_bf, as_bf(row // nq == col // nq))
    padded = jnp.floor((valid + 15.0) * (1.0 / 16.0)) * 16.0
    begin = dot(padded.astype(BF16), as_bf((row // nq < col // nq) & (row % nq == 0))) + in_dev
    first = begin[0:1].astype(jnp.int32)
    end = (begin + counts)[0:1].astype(jnp.int32)
    where = iota((tiles * 256, n), 0)
    seg[...] = as_bf((where >= first) & (where < end))

    total = jnp.zeros((nd, n), F32)
    for t in range(tiles):
        value = best[t]
        high = value.astype(BF16)
        rest = value - high.astype(F32)
        mid = rest.astype(BF16)
        low = (rest - mid.astype(F32)).astype(BF16)
        part = dot(jnp.concatenate([high, mid, low], axis=0), seg[t * 256:(t + 1) * 256, :])
        total = total + ((part[0:nd] + part[nd:2 * nd]) + part[2 * nd:3 * nd])
    mine = scores.at[pl.ds(me * nd, nd)]
    scores[pl.ds(me * nd, nd), :] = total
    pl.semaphore_wait(barrier, 7)
    copies = [pltpu.make_async_remote_copy(src_ref=mine, dst_ref=mine, send_sem=send_sem.at[rel - 1],
                                           recv_sem=recv_sem.at[rel - 1], device_id=place(rel)[0], device_id_type=MESH)
              for rel in (6, 7, 2, 3, 4, 5, 1)]
    for copy in copies:
        copy.start()
    for rel in range(1, 8):
        theirs = scores.at[pl.ds(place(rel)[1] * nd, nd)]
        pltpu.make_async_remote_copy(src_ref=theirs, dst_ref=theirs, send_sem=send_sem.at[rel - 1],
                                     recv_sem=recv_sem.at[rel - 1], device_id=place(rel)[0],
                                     device_id_type=MESH).wait_recv()

    logits = scores[...] / temp[0]
    own = jnp.sum(jnp.where(row == col, logits, 0.0), axis=0, keepdims=True)
    peak = jnp.max(logits, axis=0, keepdims=True)
    loss = jnp.log(jnp.sum(jnp.exp(logits - peak), axis=0, keepdims=True)) + peak - own
    mean[...] = jnp.sum(loss, axis=1, keepdims=True) / n
    small_row, small_col = iota((nq, n), 0), iota((nq, n), 1)
    picked = jnp.sum(jnp.where(small_col == me * nq + small_row, loss, 0.0), axis=1, keepdims=True)
    losses[...] = jnp.sum(jnp.where(small_col == small_row, picked, 0.0), axis=0, keepdims=True)[:, 0:nq]
    for copy in copies:
        copy.wait_send()


VMEM = pl.BlockSpec(memory_space=pltpu.VMEM)
SMEM = pl.BlockSpec(memory_space=pltpu.SMEM)
ANY = pl.BlockSpec(memory_space=pl.ANY)
DMA = pltpu.SemaphoreType.DMA


def solution(mesh):
    def local_step(query_hidden, doc_hidden, w_proj, query_mask, doc_mask, temperature):
        nq, qlen, hidden = query_hidden.shape
        nd, dlen, _ = doc_hidden.shape
        rows = nq * qlen
        tiles = rows * 8 // 256
        hbm = lambda x: pltpu.with_memory_space_constraint(x, pltpu.HBM)
        vmem = lambda x: pltpu.with_memory_space_constraint(x, pltpu.VMEM)
        q_all, qm_all, p_ext, table = pl.pallas_call(
            functools.partial(project_kernel, nq, qlen, nd, dlen),
            out_shape=[
                pltpu.VMEM((rows * 8, 128), BF16),
                pltpu.VMEM((nq * 8, qlen), jnp.int32),
                pltpu.VMEM((nd * dlen, 256), BF16),
                pltpu.VMEM((8, 256), jnp.int32),
            ],
            in_specs=[ANY] * 5,
            out_specs=[VMEM] * 4,
            scratch_shapes=[
                pltpu.VMEM((rows, hidden), BF16),
                pltpu.VMEM((hidden, 128), BF16),
                pltpu.VMEM((nd, dlen), jnp.int32),
                pltpu.VMEM((dlen, 128), BF16),
                pltpu.VMEM((RING, dlen, hidden), BF16),
                DMA((4,)), DMA((RING,)), DMA((7,)), DMA((7,)), DMA((7,)), DMA((7,)),
            ],
            compiler_params=pltpu.CompilerParams(collective_id=0, has_side_effects=True, vmem_limit_bytes=50 * 2**20),
            name='project',
        )(hbm(query_hidden.reshape(rows, hidden)), hbm(doc_hidden.reshape(nd * dlen, hidden)), hbm(w_proj),
          hbm(query_mask), hbm(doc_mask))

        best = pl.pallas_call(
            functools.partial(score_kernel, nd, rows, tiles),
            out_shape=pltpu.VMEM((tiles, nd, 256), F32),
            in_specs=[SMEM, VMEM, VMEM],
            out_specs=VMEM,
            scratch_shapes=[
                pltpu.VMEM((rows * 8 + 512, 128), BF16),
                pltpu.VMEM((tiles + 1, nd, 8, 256), F32),
                pltpu.VMEM((tiles + 1, nd, 8, 256), F32),
            ],
            compiler_params=pltpu.CompilerParams(vmem_limit_bytes=30 * 2**20),
            name='score',
        )(table, vmem(q_all), vmem(p_ext))

        losses, mean = pl.pallas_call(
            functools.partial(loss_kernel, nq, nd, qlen, tiles),
            out_shape=[jax.ShapeDtypeStruct((1, nq), F32), jax.ShapeDtypeStruct((1, 1), F32)],
            in_specs=[SMEM, VMEM, VMEM],
            out_specs=[VMEM, VMEM],
            scratch_shapes=[
                pltpu.VMEM((tiles * 256, nq * 8), BF16),
                pltpu.VMEM((nd * 8, nq * 8), F32),
                DMA((7,)), DMA((7,)),
            ],
            compiler_params=pltpu.CompilerParams(collective_id=1, has_side_effects=True),
            name='loss',
        )(temperature.reshape(1), vmem(best), vmem(qm_all))
        return losses.reshape(nq), mean.reshape(1)

    tok, mask, row = P(('replica', 'data2', 'data'), None, None), P(('replica', 'data2', 'data'), None), P(('replica', 'data2', 'data'))
    return jax.shard_map(local_step, mesh=mesh, in_specs=(tok, tok, P(None, None), mask, mask, P()),
                         out_specs=(row, P('replica')), check_vma=False)
```

time: 149 us -> 54.3 us (0.36); the launches traced: 148 us -> 55.3 us
  matrix products: 65.8 us -> 0 us
  Pallas kernels: 0 us -> 51.1 us
  blocking collectives: 40.4 us -> 0 us
  between operations: 16.6 us -> 3.06 us
  other arithmetic: 9.91 us -> 0 us
  local copies, waits for them, and re-layouts: 8.62 us -> 1.14 us
  starting transfers between devices: 3.26 us -> 0 us
  waiting for transfers between devices: 2.96 us -> 0 us
    dot_general x10 -> x0, matrix products: 65.8 us -> none  [the longest x8 43.9 us: tile_scores(): jnp.einsum('qtc,jsc->qtjs', q_block, p_block, preferred_element_type=jnp....]
    pallas_call x0 -> x3, Pallas kernels: none -> 51.1 us  [the longest x1 22.6 us: local_step(): pl.pallas_call(functools.partial(project_kernel, nq, qlen, nd, dlen), out...]
    psum x1 -> x0, blocking collectives: 22.4 us -> none  [local_step(): mean_loss = lax.psum(jnp.sum(losses), batch_axes) / total_batch]
    all_gather x1 -> x0, blocking collectives: 11.9 us -> none  [local_step(): q_all = lax.all_gather(q_vecs, 'data', axis=0, tiled=True)]
    all_to_all x1 -> x0, blocking collectives: 6.15 us -> none  [local_step(): column = lax.all_to_all(column, 'data', 1, 1, tiled=True)]
    convert_element_type x1 -> x0, other arithmetic: 5.11 us -> none  [project_norm(): return (projected / jnp.maximum(norm_len, 1e-12)).astype(jnp.bfloat16)]
    while x1 -> x0, local copies, waits for them, and re-layouts: 4.64 us -> none  [local_step(): lax.map(lambda q_block: tile_scores(q_block, p_vecs, doc_valid), q_blocks)]
    all_to_all x1 -> x0, starting transfers between devices: 3.22 us -> none  [local_step(): column = lax.all_to_all(column, 'data2', 0, 0, tiled=True)]
  transfers between devices with their start and end apart: 2 -> 0, of which waited for: 1 -> 0; matrix products, arithmetic and copies ran while one was open for 20% -> 0% of each run, Pallas kernels for 0% -> 0%
where the time goes in v1:
time: 54.3 us; the launch traced here: 55.3 us
  Pallas kernels  51.1 us (94%)
  between operations  3.06 us (6%)
  local copies, waits for them, and re-layouts  1.14 us (2%)
    pallas_call x1, Pallas kernels, local_step(): pl.pallas_call(functools.partial(project_kernel, nq, qlen, nd, dlen), out...  22.6 us
    pallas_call x1, Pallas kernels, local_step(): pl.pallas_call(functools.partial(score_kernel, nd, rows, tiles), out_shap...  19.6 us
    pallas_call x1, Pallas kernels, local_step(): pl.pallas_call(functools.partial(loss_kernel, nq, nd, qlen, tiles), out_s...  9.01 us
    unnamed x1, local copies, waits for them, and re-layouts  1.14 us

profile of v1, /device:TPU:0, one launch (start us, length us, event | category | flops | bytes accessed | tf_op | source)
XLA Modules:
  0.0 55.3 jit_solution(6793302060079688335)
XLA Ops:
  0.6 22.6 %project.1 = (bf16[4096,128]{1,0:T(8,128)(2,1)S(1)}, s32[128,32]{1,0:T(8,128)S(1)}, bf16[12288,256]{1,0:T(8,128)(2,1)S(1)}, s32[8,256]{1,0:T(8,128)S(1)}) custom-call(bf16[512,1536]{1,0:T(8,128)(2,1)} %bitcast.7, bf16[12288,1536]{1,0:T(8,128)(2,1)} %bitcast.6, bf16[1536,128]{1,0:T(8,128)(2,1)} %w_hbm.1, s32[16,32]{1,0:T(8,128)} %qm_hbm.1, s32[16,768]{1,0:T(8,128)} %dm_hbm.1), custom_call_target="tpu_custom_call" | custom-call | tf_op jit(solution)/shard_map/project/pallas_call | solution.py:295
  23.2 19.6 %score.1.best = f32[16,16,256]{2,1,0:T(8,128)S(1)} custom-call(s32[8,256]{1,0:T(8,128)S(1)} %get-tuple-element.8.table, bf16[4096,128]{1,0:T(8,128)(2,1)S(1)} %get-tuple-element.9.q_all, bf16[12288,256]{1,0:T(8,128)(2,1)S(1)} %get-tuple-element.10.p_ext), custom_call_target="tpu_custom_call" | custom-call | tf_op jit(solution)/shard_map/score/pallas_call | solution.py:318
  43.4 9.0 %loss.1 = (f32[1,16]{1,0:T(1,128)}, f32[1,1]{1,0:T(1,128)}) custom-call(f32[1]{0:T(128)} %bitcast.5.temp, f32[16,16,256]{2,1,0:T(8,128)S(1)} %score.1.best, s32[128,32]{1,0:T(8,128)S(1)} %get-tuple-element.11.qm_all), custom_call_target="tpu_custom_call" | custom-call | tf_op jit(solution)/shard_map/loss/pallas_call | solution.py:332
  52.4 1.1 %copy.11 = f32[16]{0:T(128)} copy(f32[16]{0:T(128)} %bitcast.8) | data formatting | bytes 128

commit v2 on v1

--- a/solution.py
+++ b/solution.py
@@ -37,13 +37,14 @@
     return (projected * lax.rsqrt(jnp.maximum(square, 1e-24))).astype(BF16)
 
 
-def project_kernel(nq, qlen, nd, dlen, q_hbm, d_hbm, w_hbm, qm_hbm, dm_hbm, q_all, qm_all, p_ext, table,
-                   q_buf, w_buf, dm_buf, nmt, d_buf, in_sem, d_sem, qs_sem, qr_sem, ms_sem, mr_sem):
+def project_kernel(nq, qlen, nd, dlen, q_hbm, d_hbm, w_hbm, qm_hbm, dm_hbm, q_all, p_ext, table, seg,
+                   qm_all, q_buf, w_buf, dm_buf, nmt, d_buf, in_sem, d_sem, qs_sem, qr_sem, ms_sem, mr_sem):
     rows = nq * qlen
+    n = nq * 8
     me = place(0)[1]
-    my_mask = qm_all.at[pl.ds(me * nq, nq)]
+    as_bf = lambda cond: cond.astype(F32).astype(BF16)
     ins = [pltpu.make_async_copy(src, dst, in_sem.at[k]) for k, (src, dst) in enumerate(
-        [(qm_hbm, my_mask), (dm_hbm, dm_buf), (w_hbm, w_buf), (q_hbm, q_buf)])]
+        [(qm_hbm, qm_all.at[pl.ds(me * nq, nq)]), (dm_hbm, dm_buf), (w_hbm, w_buf), (q_hbm, q_buf)])]
     for copy in ins:
         copy.start()
 
@@ -54,17 +55,44 @@
         doc_copy(j, j).start()
 
     barrier = pltpu.get_barrier_semaphore()
-    for rel in (1, 2, 4, 6):
+    for rel in range(1, 8):
         pl.semaphore_signal(barrier, inc=1, device_id=place(rel)[0], device_id_type=MESH)
 
+    def remote(ref, per, origin_rel, to_rel, send_sem, recv_sem):
+        block = ref.at[pl.ds(place(origin_rel)[1] * per, per)]
+        return pltpu.make_async_remote_copy(src_ref=block, dst_ref=block, send_sem=send_sem, recv_sem=recv_sem,
+                                            device_id=place(to_rel)[0], device_id_type=MESH)
+
     ins[0].wait()
+    pl.semaphore_wait(barrier, 7)
+    mask_sent = [remote(qm_all, nq, 0, rel, ms_sem.at[rel - 1], mr_sem.at[rel - 1]) for rel in (6, 7, 2, 3, 4, 5, 1)]
+    for copy in mask_sent:
+        copy.start()
+
     mask = qm_all[pl.ds(me * nq, nq), :].astype(F32).astype(BF16)
-    spread = dot(mask, (iota((qlen, rows), 1) % qlen == iota((qlen, rows), 0)).astype(F32).astype(BF16))
+    spread = dot(mask, as_bf(iota((qlen, rows), 1) % qlen == iota((qlen, rows), 0)))
     flat = jnp.sum(jnp.where(iota((nq, rows), 1) // qlen == iota((nq, rows), 0), spread, 0.0), axis=0, keepdims=True)
-    before = (iota((rows, rows), 0) < iota((rows, rows), 1)).astype(F32).astype(BF16)
+    before = as_bf(iota((rows, rows), 0) < iota((rows, rows), 1))
     rank = dot(jnp.broadcast_to(flat, (16, rows)).astype(BF16), before)[0:1]
     rank = jnp.where(flat > 0.5, rank, -1.0).astype(jnp.int32)
-    pick = (iota((rows, rows), 0) == rank).astype(F32).astype(BF16)
+    pick = as_bf(iota((rows, rows), 0) == rank)
+
+    ins[2].wait()
+    ins[3].wait()
+    q_vec = unit_rows(dot(q_buf[...], w_buf[...]))
+    q_all[pl.ds(me * rows, rows), :] = dot(pick, q_vec).astype(BF16)
+    sent = []
+
+    def send(origin_rel, to_rel):
+        copy = remote(q_all, rows, origin_rel, to_rel, qs_sem.at[len(sent)], qr_sem.at[(origin_rel ^ to_rel) - 1])
+        copy.start()
+        sent.append(copy)
+
+    def received(rel):
+        remote(q_all, rows, rel, rel, qs_sem.at[0], qr_sem.at[rel - 1]).wait_recv()
+
+    for rel in (2, 4, 6, 1):
+        send(0, rel)
 
     ins[1].wait()
     dmask = dm_buf[...]
@@ -74,7 +102,7 @@
     per_doc = dlen // UNIT
     count = jnp.floor((last + (UNIT - 1.0)) * (1.0 / UNIT))
     wide = jnp.broadcast_to(count, (nd, 128))
-    upto = dot((iota((nd, nd), 0) >= iota((nd, nd), 1)).astype(F32).astype(BF16), wide.astype(BF16))[:, 0:1]
+    upto = dot(as_bf(iota((nd, nd), 0) >= iota((nd, nd), 1)), wide.astype(BF16))[:, 0:1]
     total = jnp.max(upto, axis=0, keepdims=True)
     slot_id = jnp.minimum(iota((nd, 256), 1).astype(F32), total - 1.0)
     passed = slot_id >= upto
@@ -84,33 +112,6 @@
     table[1:2, :] = doc.astype(jnp.int32)
     table[2:3, :] = jnp.broadcast_to(total, (1, 256)).astype(jnp.int32)
 
-    ins[2].wait()
-    ins[3].wait()
-    q_vec = unit_rows(dot(q_buf[...], w_buf[...]))
-    q_all[pl.ds(me * rows, rows), :] = dot(pick, q_vec).astype(BF16)
-    pl.semaphore_wait(barrier, 4)
-
-    def send(origin_rel, to_rel, k):
-        origin = place(origin_rel)[1]
-        arrive = origin_rel ^ to_rel
-        target = place(to_rel)[0]
-        q_ref, m_ref = q_all.at[pl.ds(origin * rows, rows)], qm_all.at[pl.ds(origin * nq, nq)]
-        pair = [pltpu.make_async_remote_copy(src_ref=ref, dst_ref=ref, send_sem=ss.at[k], recv_sem=rs.at[arrive - 1],
-                                             device_id=target, device_id_type=MESH)
-                for ref, ss, rs in ((m_ref, ms_sem, mr_sem), (q_ref, qs_sem, qr_sem))]
-        for copy in pair:
-            copy.start()
-        return pair
-
-    def received(rel):
-        origin = place(rel)[1]
-        q_ref, m_ref = q_all.at[pl.ds(origin * rows, rows)], qm_all.at[pl.ds(origin * nq, nq)]
-        for ref, ss, rs in ((m_ref, ms_sem, mr_sem), (q_ref, qs_sem, qr_sem)):
-            pltpu.make_async_remote_copy(src_ref=ref, dst_ref=ref, send_sem=ss.at[0], recv_sem=rs.at[rel - 1],
-                                         device_id=place(rel)[0], device_id_type=MESH).wait_recv()
-
-    sent = [send(0, rel, k) for k, rel in enumerate((2, 4, 6, 1))]
-
     def project(j, carry):
         slot = lax.rem(j, RING)
         doc_copy(j, slot).wait()
@@ -123,28 +124,38 @@
 
         return carry
 
-    split = (5 * nd) // 8
-    lax.fori_loop(0, split, project, 0)
-    for k, rel in enumerate((2, 4)):
+    cut1, cut2 = (7 * nd) // 16, (12 * nd) // 16
+    lax.fori_loop(0, cut1, project, 0)
+    for rel in (2, 4):
         received(rel)
-        sent.append(send(rel, 1, 4 + k))
-    lax.fori_loop(split, nd, project, 0)
+        send(rel, 1)
+
+    for rel in range(1, 8):
+        remote(qm_all, nq, rel, rel, ms_sem.at[rel - 1], mr_sem.at[rel - 1]).wait_recv()
+    row, col = iota((n, n), 0), iota((n, n), 1)
+    every = qm_all[...].astype(F32).astype(BF16)
+    counts = lax.dot_general(jnp.ones((16, qlen), BF16), every, (((1,), (1,)), ((), ())), preferred_element_type=F32)
+    counts_bf = counts.astype(BF16)
+    in_dev = dot(counts_bf, as_bf((row // nq == col // nq) & (row < col)))
+    padded = jnp.floor((dot(counts_bf, as_bf(row // nq == col // nq)) + 15.0) * (1.0 / 16.0)) * 16.0
+    padded_bf = padded.astype(BF16)
+    begin = dot(padded_bf, as_bf((row // nq < col // nq) & (row % nq == 0))) + in_dev
+    starts = dot(padded_bf, as_bf((row // nq < col) & (row % nq == 0)))
+    table[3:4, 0:128] = starts[0:1].astype(jnp.int32)
+    table[3:4, 128:256] = starts[0:1].astype(jnp.int32)
+    first = begin[0:1].astype(jnp.int32)
+    end = (begin + counts)[0:1].astype(jnp.int32)
+    where = iota((rows * 8, n), 0)
+    seg[...] = as_bf((where >= first) & (where < end))
+
+    lax.fori_loop(cut1, cut2, project, 0)
     received(6)
-    sent.append(send(6, 1, 6))
+    send(6, 1)
+    lax.fori_loop(cut2, nd, project, 0)
     for rel in (1, 3, 5, 7):
         received(rel)
-
-    lane = iota((1, 256), 1)
-    start = jnp.zeros((1, 1), jnp.int32)
-    starts = jnp.zeros((1, 256), jnp.int32)
-    for dev in range(8):
-        starts = starts + jnp.where(lane == dev, start, 0)
-        valid = jnp.sum(jnp.sum(qm_all[dev * nq:(dev + 1) * nq, :].astype(F32), axis=1, keepdims=True), axis=0, keepdims=True)
-        start = start + (jnp.floor((valid + 15.0) * (1.0 / 16.0)) * 16.0).astype(jnp.int32)
-    table[3:4, :] = starts + jnp.where(lane == 8, start, 0)
-    for pair in sent:
-        for copy in pair:
-            copy.wait_send()
+    for copy in mask_sent + sent:
+        copy.wait_send()
 
 
 def score_body(nd, rows, tiles, table, q_all, p_ext, out, q_list, best, accs):
@@ -221,29 +232,12 @@
     pl.run_scoped(body, *[pltpu.ACC(0)((UNIT, 256), F32)] * LANES, *[pltpu.ACC(1)((UNIT, 256), F32)] * LANES)
 
 
-def loss_kernel(nq, nd, qlen, tiles, temp, best, qm_all, losses, mean, seg, scores, send_sem, recv_sem):
-    n = nq * 8
+def gather_kernel(nd, tiles, temp, best, seg, scores, send_sem, recv_sem):
     me = place(0)[1]
     barrier = pltpu.get_barrier_semaphore()
     for rel in range(1, 8):
         pl.semaphore_signal(barrier, inc=1, device_id=place(rel)[0], device_id_type=MESH)
-
-    col = iota((n, n), 1)
-    row = iota((n, n), 0)
-    as_bf = lambda cond: cond.astype(F32).astype(BF16)
-    mask = qm_all[...].astype(F32).astype(BF16)
-    counts = lax.dot_general(jnp.ones((16, qlen), BF16), mask, (((1,), (1,)), ((), ())), preferred_element_type=F32)
-    counts_bf = counts.astype(BF16)
-    in_dev = dot(counts_bf, as_bf((row // nq == col // nq) & (row < col)))
-    valid = dot(counts_bf, as_bf(row // nq == col // nq))
-    padded = jnp.floor((valid + 15.0) * (1.0 / 16.0)) * 16.0
-    begin = dot(padded.astype(BF16), as_bf((row // nq < col // nq) & (row % nq == 0))) + in_dev
-    first = begin[0:1].astype(jnp.int32)
-    end = (begin + counts)[0:1].astype(jnp.int32)
-    where = iota((tiles * 256, n), 0)
-    seg[...] = as_bf((where >= first) & (where < end))
-
-    total = jnp.zeros((nd, n), F32)
+    total = jnp.zeros((nd, nd * 8), F32)
     for t in range(tiles):
         value = best[t]
         high = value.astype(BF16)
@@ -252,30 +246,34 @@
         low = (rest - mid.astype(F32)).astype(BF16)
         part = dot(jnp.concatenate([high, mid, low], axis=0), seg[t * 256:(t + 1) * 256, :])
         total = total + ((part[0:nd] + part[nd:2 * nd]) + part[2 * nd:3 * nd])
-    mine = scores.at[pl.ds(me * nd, nd)]
-    scores[pl.ds(me * nd, nd), :] = total
+    scores[pl.ds(me * nd, nd), :] = total / temp[0]
     pl.semaphore_wait(barrier, 7)
-    copies = [pltpu.make_async_remote_copy(src_ref=mine, dst_ref=mine, send_sem=send_sem.at[rel - 1],
-                                           recv_sem=recv_sem.at[rel - 1], device_id=place(rel)[0], device_id_type=MESH)
-              for rel in (6, 7, 2, 3, 4, 5, 1)]
+
+    def remote(origin_rel, rel):
+        block = scores.at[pl.ds(place(origin_rel)[1] * nd, nd)]
+        return pltpu.make_async_remote_copy(src_ref=block, dst_ref=block, send_sem=send_sem.at[rel - 1],
+                                            recv_sem=recv_sem.at[rel - 1], device_id=place(rel)[0], device_id_type=MESH)
+
+    copies = [remote(0, rel) for rel in (6, 7, 2, 3, 4, 5, 1)]
     for copy in copies:
         copy.start()
     for rel in range(1, 8):
-        theirs = scores.at[pl.ds(place(rel)[1] * nd, nd)]
-        pltpu.make_async_remote_copy(src_ref=theirs, dst_ref=theirs, send_sem=send_sem.at[rel - 1],
-                                     recv_sem=recv_sem.at[rel - 1], device_id=place(rel)[0],
-                                     device_id_type=MESH).wait_recv()
-
-    logits = scores[...] / temp[0]
-    own = jnp.sum(jnp.where(row == col, logits, 0.0), axis=0, keepdims=True)
+        remote(rel, rel).wait_recv()
+    for copy in copies:
+        copy.wait_send()
+
+
+def loss_kernel(nq, scores, losses, mean):
+    n = nq * 8
+    me = place(0)[1]
+    logits = scores[...]
+    own = jnp.sum(jnp.where(iota((n, n), 0) == iota((n, n), 1), logits, 0.0), axis=0, keepdims=True)
     peak = jnp.max(logits, axis=0, keepdims=True)
     loss = jnp.log(jnp.sum(jnp.exp(logits - peak), axis=0, keepdims=True)) + peak - own
     mean[...] = jnp.sum(loss, axis=1, keepdims=True) / n
-    small_row, small_col = iota((nq, n), 0), iota((nq, n), 1)
-    picked = jnp.sum(jnp.where(small_col == me * nq + small_row, loss, 0.0), axis=1, keepdims=True)
-    losses[...] = jnp.sum(jnp.where(small_col == small_row, picked, 0.0), axis=0, keepdims=True)[:, 0:nq]
-    for copy in copies:
-        copy.wait_send()
+    row, col = iota((nq, n), 0), iota((nq, n), 1)
+    picked = jnp.sum(jnp.where(col == me * nq + row, loss, 0.0), axis=1, keepdims=True)
+    losses[...] = jnp.sum(jnp.where(col == row, picked, 0.0), axis=0, keepdims=True)[:, 0:nq]
 
 
 VMEM = pl.BlockSpec(memory_space=pltpu.VMEM)
@@ -292,17 +290,18 @@
         tiles = rows * 8 // 256
         hbm = lambda x: pltpu.with_memory_space_constraint(x, pltpu.HBM)
         vmem = lambda x: pltpu.with_memory_space_constraint(x, pltpu.VMEM)
-        q_all, qm_all, p_ext, table = pl.pallas_call(
+        q_all, p_ext, table, seg = pl.pallas_call(
             functools.partial(project_kernel, nq, qlen, nd, dlen),
             out_shape=[
                 pltpu.VMEM((rows * 8, 128), BF16),
-                pltpu.VMEM((nq * 8, qlen), jnp.int32),
                 pltpu.VMEM((nd * dlen, 256), BF16),
                 pltpu.VMEM((8, 256), jnp.int32),
+                pltpu.VMEM((rows * 8, nq * 8), BF16),
             ],
             in_specs=[ANY] * 5,
             out_specs=[VMEM] * 4,
             scratch_shapes=[
+                pltpu.VMEM((nq * 8, qlen), jnp.int32),
                 pltpu.VMEM((rows, hidden), BF16),
                 pltpu.VMEM((hidden, 128), BF16),
                 pltpu.VMEM((nd, dlen), jnp.int32),
@@ -329,19 +328,23 @@
             name='score',
         )(table, vmem(q_all), vmem(p_ext))
 
+        scores = pl.pallas_call(
+            functools.partial(gather_kernel, nd, tiles),
+            out_shape=pltpu.VMEM((nd * 8, nq * 8), F32),
+            in_specs=[SMEM, VMEM, VMEM],
+            out_specs=VMEM,
+            scratch_shapes=[DMA((7,)), DMA((7,))],
+            compiler_params=pltpu.CompilerParams(collective_id=1, has_side_effects=True),
+            name='gather',
+        )(temperature.reshape(1), vmem(best), vmem(seg))
+
         losses, mean = pl.pallas_call(
-            functools.partial(loss_kernel, nq, nd, qlen, tiles),
+            functools.partial(loss_kernel, nq),
             out_shape=[jax.ShapeDtypeStruct((1, nq), F32), jax.ShapeDtypeStruct((1, 1), F32)],
-            in_specs=[SMEM, VMEM, VMEM],
+            in_specs=[VMEM],
             out_specs=[VMEM, VMEM],
-            scratch_shapes=[
-                pltpu.VMEM((tiles * 256, nq * 8), BF16),
-                pltpu.VMEM((nd * 8, nq * 8), F32),
-                DMA((7,)), DMA((7,)),
-            ],
-            compiler_params=pltpu.CompilerParams(collective_id=1, has_side_effects=True),
             name='loss',
-        )(temperature.reshape(1), vmem(best), vmem(qm_all))
+        )(vmem(scores))
         return losses.reshape(nq), mean.reshape(1)
 
     tok, mask, row = P(('replica', 'data2', 'data'), None, None), P(('replica', 'data2', 'data'), None), P(('replica', 'data2', 'data'))

time: 54.3 us -> 51.6 us (0.950); the launches traced: 55.3 us -> 51.4 us
  between operations: 3.06 us -> 1.3 us
  local copies, waits for them, and re-layouts: 1.14 us -> 0 us
  Pallas kernels: 51.1 us -> 50.1 us
    pallas_call x1 -> x2, Pallas kernels: 9.01 us -> 5.38 us  [the longest x1 4.73 us: local_step(): pl.pallas_call(functools.partial(gather_kernel, nd, tiles), out_shape=plt...]
    pallas_call x1, Pallas kernels: 19.6 us -> 21.3 us  [local_step(): pl.pallas_call(functools.partial(score_kernel, nd, rows, tiles), out_shap...]
    unnamed x1 -> x0, local copies, waits for them, and re-layouts: 1.14 us -> none
    pallas_call x1, Pallas kernels: 22.6 us -> 23.5 us  [local_step(): pl.pallas_call(functools.partial(project_kernel, nq, qlen, nd, dlen), out...]
where the time goes in v2:
time: 51.6 us; the launch traced here: 51.4 us
  Pallas kernels  50.1 us (97%)
  between operations  1.3 us (3%)
    pallas_call x1, Pallas kernels, local_step(): pl.pallas_call(functools.partial(project_kernel, nq, qlen, nd, dlen), out...  23.5 us
    pallas_call x1, Pallas kernels, local_step(): pl.pallas_call(functools.partial(score_kernel, nd, rows, tiles), out_shap...  21.3 us
    pallas_call x1, Pallas kernels, local_step(): pl.pallas_call(functools.partial(gather_kernel, nd, tiles), out_shape=plt...  4.73 us

profile of v2, /device:TPU:0, one launch (start us, length us, event | category | flops | bytes accessed | tf_op | source)
XLA Modules:
  0.0 51.4 jit_solution(9075365471690886498)
XLA Ops:
  0.6 23.5 %project.1 = (bf16[4096,128]{1,0:T(8,128)(2,1)S(1)}, bf16[12288,256]{1,0:T(8,128)(2,1)S(1)}, s32[8,256]{1,0:T(8,128)S(1)}, bf16[4096,128]{1,0:T(8,128)(2,1)S(1)}) custom-call(bf16[512,1536]{1,0:T(8,128)(2,1)} %bitcast.7, bf16[12288,1536]{1,0:T(8,128)(2,1)} %bitcast.6, bf16[1536,128]{1,0:T(8,128)(2,1)} %w_hbm.1, s32[16,32]{1,0:T(8,128)} %qm_hbm.1, ...), custom_call_target="tpu_custom_call" | custom-call | tf_op jit(solution)/shard_map/project/pallas_call | solution.py:293
  24.1 21.3 %score.1.best = f32[16,16,256]{2,1,0:T(8,128)S(1)} custom-call(s32[8,256]{1,0:T(8,128)S(1)} %get-tuple-element.8.table, bf16[4096,128]{1,0:T(8,128)(2,1)S(1)} %get-tuple-element.9.q_all, bf16[12288,256]{1,0:T(8,128)(2,1)S(1)} %get-tuple-element.10.p_ext), custom_call_target="tpu_custom_call" | custom-call | tf_op jit(solution)/shard_map/score/pallas_call | solution.py:317
  46.0 4.7 %gather.1.scores = f32[128,128]{1,0:T(8,128)S(1)} custom-call(f32[1]{0:T(128)} %bitcast.5.temp, f32[16,16,256]{2,1,0:T(8,128)S(1)} %score.1.best, bf16[4096,128]{1,0:T(8,128)(2,1)S(1)} %get-tuple-element.11.seg), custom_call_target="tpu_custom_call" | custom-call | tf_op jit(solution)/shard_map/gather/pallas_call | solution.py:331
  50.8 0.7 %loss.1 = (f32[1,16]{1,0:T(1,128)}, f32[1,1]{1,0:T(1,128)}) custom-call(f32[128,128]{1,0:T(8,128)S(1)} %gather.1.scores), custom_call_target="tpu_custom_call" | custom-call | tf_op jit(solution)/shard_map/loss/pallas_call | solution.py:341

commit v3 on v2

--- a/solution.py
+++ b/solution.py
@@ -12,7 +12,10 @@
 BIG = 1e30
 UNIT = 64
 LANES = 8
-RING = 6
+RING = 4
+HEAD = 256
+GROUP = 4
+TAIL_RING = 8
 
 
 def iota(shape, dim):
@@ -37,8 +40,12 @@
     return (projected * lax.rsqrt(jnp.maximum(square, 1e-24))).astype(BF16)
 
 
-def project_kernel(nq, qlen, nd, dlen, q_hbm, d_hbm, w_hbm, qm_hbm, dm_hbm, q_all, p_ext, table, seg,
-                   qm_all, q_buf, w_buf, dm_buf, nmt, d_buf, in_sem, d_sem, qs_sem, qr_sem, ms_sem, mr_sem):
+def mask_features(doc, off):
+    return jnp.where(iota(off.shape, 1) == doc, off.astype(F32), 0.0).astype(BF16)
+
+
+def project_kernel(nq, qlen, nd, dlen, q_hbm, d_hbm, w_hbm, qm_hbm, dm_hbm, q_all, p_ext, table, seg, nmt,
+                   qm_all, q_buf, w_buf, dm_buf, d_buf, in_sem, d_sem, qs_sem, qr_sem, ms_sem, mr_sem):
     rows = nq * qlen
     n = nq * 8
     me = place(0)[1]
@@ -49,7 +56,7 @@
         copy.start()
 
     def doc_copy(j, slot):
-        return pltpu.make_async_copy(d_hbm.at[pl.ds(j * dlen, dlen)], d_buf.at[slot], d_sem.at[slot])
+        return pltpu.make_async_copy(d_hbm.at[pl.ds(j * dlen, HEAD)], d_buf.at[slot], d_sem.at[slot])
 
     for j in range(RING):
         doc_copy(j, j).start()
@@ -101,22 +108,27 @@
     last = jnp.max(dmask * (iota((nd, dlen), 1) + 1), axis=1, keepdims=True).astype(F32)
     per_doc = dlen // UNIT
     count = jnp.floor((last + (UNIT - 1.0)) * (1.0 / UNIT))
-    wide = jnp.broadcast_to(count, (nd, 128))
-    upto = dot(as_bf(iota((nd, nd), 0) >= iota((nd, nd), 1)), wide.astype(BF16))[:, 0:1]
-    total = jnp.max(upto, axis=0, keepdims=True)
-    slot_id = jnp.minimum(iota((nd, 256), 1).astype(F32), total - 1.0)
-    passed = slot_id >= upto
-    unit = slot_id[0:1] + jnp.sum(jnp.where(passed, per_doc - count, 0.0), axis=0, keepdims=True)
-    doc = jnp.sum(jnp.where(passed, 1.0, 0.0), axis=0, keepdims=True)
-    table[0:1, :] = unit.astype(jnp.int32)
-    table[1:2, :] = doc.astype(jnp.int32)
-    table[2:3, :] = jnp.broadcast_to(total, (1, 256)).astype(jnp.int32)
+    sums = as_bf(iota((nd, nd), 0) >= iota((nd, nd), 1))
+
+    def listing(at, count, first):
+        upto = dot(sums, jnp.broadcast_to(count, (nd, 128)).astype(BF16))[:, 0:1]
+        total = jnp.max(upto, axis=0, keepdims=True)
+        slot_id = jnp.minimum(iota((nd, 256), 1).astype(F32), jnp.maximum(total - 1.0, 0.0))
+        passed = slot_id >= upto
+        unit = slot_id[0:1] + first + jnp.sum(jnp.where(passed, per_doc - count, 0.0), axis=0, keepdims=True)
+        doc = jnp.sum(jnp.where(passed, 1.0, 0.0), axis=0, keepdims=True)
+        table[at:at + 1, :] = unit.astype(jnp.int32)
+        table[at + 1:at + 2, :] = doc.astype(jnp.int32)
+        table[at + 2:at + 3, :] = jnp.broadcast_to(total, (1, 256)).astype(jnp.int32)
+
+    listing(0, count, 0.0)
+    listing(4, jnp.maximum(count - HEAD // UNIT, 0.0), float(HEAD // UNIT))
 
     def project(j, carry):
         slot = lax.rem(j, RING)
         doc_copy(j, slot).wait()
-        p_ext[pl.ds(j * dlen, dlen), 0:128] = unit_rows(dot(d_buf[slot], w_buf[...]))
-        p_ext[pl.ds(j * dlen, dlen), 128:256] = jnp.where(iota((dlen, 128), 1) == j, nmt[...].astype(F32), 0.0).astype(BF16)
+        p_ext[pl.ds(j * dlen, HEAD), 0:128] = unit_rows(dot(d_buf[slot], w_buf[...]))
+        p_ext[pl.ds(j * dlen, HEAD), 128:256] = mask_features(j, nmt[0:HEAD, :])
 
         @pl.when(j + RING < nd)
         def _():
@@ -124,8 +136,7 @@
 
         return carry
 
-    cut1, cut2 = (7 * nd) // 16, (12 * nd) // 16
-    lax.fori_loop(0, cut1, project, 0)
+    lax.fori_loop(0, nd, project, 0)
     for rel in (2, 4):
         received(rel)
         send(rel, 1)
@@ -148,14 +159,46 @@
     where = iota((rows * 8, n), 0)
     seg[...] = as_bf((where >= first) & (where < end))
 
-    lax.fori_loop(cut1, cut2, project, 0)
     received(6)
     send(6, 1)
-    lax.fori_loop(cut2, nd, project, 0)
     for rel in (1, 3, 5, 7):
         received(rel)
     for copy in mask_sent + sent:
         copy.wait_send()
+
+
+def tail_kernel(per_doc, table, d_hbm, w, nmt, p_head, p_ext, d_buf, sem):
+    steps = (table[6, 0] + (GROUP - 1)) // GROUP
+
+    def copies(g):
+        slot = lax.rem(g, TAIL_RING)
+        return [pltpu.make_async_copy(d_hbm.at[pl.ds(pl.multiple_of(table[4, g * GROUP + k] * UNIT, UNIT), UNIT)],
+                                      d_buf.at[slot, pl.ds(k * UNIT, UNIT)], sem.at[slot]) for k in range(GROUP)]
+
+    for g in range(TAIL_RING):
+        @pl.when(g < steps)
+        def _():
+            for copy in copies(g):
+                copy.start()
+
+    def step(g, carry):
+        for copy in copies(g):
+            copy.wait()
+        value = unit_rows(dot(d_buf[lax.rem(g, TAIL_RING)], w[...]))
+        for k in range(GROUP):
+            unit, doc = table[4, g * GROUP + k], table[5, g * GROUP + k]
+            at = pl.ds(pl.multiple_of(unit * UNIT, UNIT), UNIT)
+            p_ext[at, 0:128] = value[k * UNIT:(k + 1) * UNIT]
+            p_ext[at, 128:256] = mask_features(doc, nmt[pl.ds(pl.multiple_of((unit - doc * per_doc) * UNIT, UNIT), UNIT), :])
+
+        @pl.when(g + TAIL_RING < steps)
+        def _():
+            for copy in copies(g + TAIL_RING):
+                copy.start()
+
+        return carry
+
+    lax.fori_loop(0, steps, step, 0)
 
 
 def score_body(nd, rows, tiles, table, q_all, p_ext, out, q_list, best, accs):
@@ -290,29 +333,40 @@
         tiles = rows * 8 // 256
         hbm = lambda x: pltpu.with_memory_space_constraint(x, pltpu.HBM)
         vmem = lambda x: pltpu.with_memory_space_constraint(x, pltpu.VMEM)
-        q_all, p_ext, table, seg = pl.pallas_call(
+        q_all, p_head, table, seg, nmt = pl.pallas_call(
             functools.partial(project_kernel, nq, qlen, nd, dlen),
             out_shape=[
                 pltpu.VMEM((rows * 8, 128), BF16),
                 pltpu.VMEM((nd * dlen, 256), BF16),
                 pltpu.VMEM((8, 256), jnp.int32),
                 pltpu.VMEM((rows * 8, nq * 8), BF16),
+                pltpu.VMEM((dlen, 128), BF16),
             ],
             in_specs=[ANY] * 5,
-            out_specs=[VMEM] * 4,
+            out_specs=[VMEM] * 5,
             scratch_shapes=[
                 pltpu.VMEM((nq * 8, qlen), jnp.int32),
                 pltpu.VMEM((rows, hidden), BF16),
                 pltpu.VMEM((hidden, 128), BF16),
                 pltpu.VMEM((nd, dlen), jnp.int32),
-                pltpu.VMEM((dlen, 128), BF16),
-                pltpu.VMEM((RING, dlen, hidden), BF16),
+                pltpu.VMEM((RING, HEAD, hidden), BF16),
                 DMA((4,)), DMA((RING,)), DMA((7,)), DMA((7,)), DMA((7,)), DMA((7,)),
             ],
-            compiler_params=pltpu.CompilerParams(collective_id=0, has_side_effects=True, vmem_limit_bytes=50 * 2**20),
+            compiler_params=pltpu.CompilerParams(collective_id=0, has_side_effects=True, vmem_limit_bytes=30 * 2**20),
             name='project',
         )(hbm(query_hidden.reshape(rows, hidden)), hbm(doc_hidden.reshape(nd * dlen, hidden)), hbm(w_proj),
           hbm(query_mask), hbm(doc_mask))
+
+        p_ext = pl.pallas_call(
+            functools.partial(tail_kernel, dlen // UNIT),
+            out_shape=pltpu.VMEM((nd * dlen, 256), BF16),
+            in_specs=[SMEM, ANY, VMEM, VMEM, VMEM],
+            out_specs=VMEM,
+            scratch_shapes=[pltpu.VMEM((TAIL_RING, GROUP * UNIT, hidden), BF16), DMA((TAIL_RING,))],
+            input_output_aliases={4: 0},
+            compiler_params=pltpu.CompilerParams(vmem_limit_bytes=30 * 2**20),
+            name='tail',
+        )(table, hbm(doc_hidden.reshape(nd * dlen, hidden)), w_proj, vmem(nmt), vmem(p_head))
 
         best = pl.pallas_call(
             functools.partial(score_kernel, nd, rows, tiles),

time: 51.6 us -> 52.6 us (1.019)
  Pallas kernels: 50.1 us -> 51.4 us
    pallas_call x0 -> x1, Pallas kernels: none -> 10 us  [local_step(): pl.pallas_call(functools.partial(tail_kernel, dlen // UNIT), out_shape=pl...]
    pallas_call x1, Pallas kernels: 23.5 us -> 16.1 us  [local_step(): pl.pallas_call(functools.partial(project_kernel, nq, qlen, nd, dlen), out...]
    pallas_call x1, Pallas kernels: 21.3 us -> 19.3 us  [local_step(): pl.pallas_call(functools.partial(score_kernel, nd, rows, tiles), out_shap...]
    pallas_call x1, Pallas kernels: 4.73 us -> 5.37 us  [local_step(): pl.pallas_call(functools.partial(gather_kernel, nd, tiles), out_shape=plt...]
where the time goes in v3:
time: 52.6 us; the launch traced here: 52.8 us
  Pallas kernels  51.4 us (98%)
  between operations  1.33 us (3%)
    pallas_call x1, Pallas kernels, local_step(): pl.pallas_call(functools.partial(score_kernel, nd, rows, tiles), out_shap...  19.3 us
    pallas_call x1, Pallas kernels, local_step(): pl.pallas_call(functools.partial(project_kernel, nq, qlen, nd, dlen), out...  16.1 us
    pallas_call x1, Pallas kernels, local_step(): pl.pallas_call(functools.partial(tail_kernel, dlen // UNIT), out_shape=pl...  10 us
    pallas_call x1, Pallas kernels, local_step(): pl.pallas_call(functools.partial(gather_kernel, nd, tiles), out_shape=plt...  5.37 us

profile of v3, /device:TPU:0, one launch (start us, length us, event | category | flops | bytes accessed | tf_op | source)
XLA Modules:
  0.0 52.8 jit_solution(5463855066261814112)
XLA Ops:
  0.6 0.0 copy-start
  0.6 16.1 %project.1 = (bf16[4096,128]{1,0:T(8,128)(2,1)S(1)}, bf16[12288,256]{1,0:T(8,128)(2,1)S(1)}, s32[8,256]{1,0:T(8,128)S(1)}, bf16[4096,128]{1,0:T(8,128)(2,1)S(1)}, bf16[768,128]{1,0:T(8,128)(2,1)S(1)}) custom-call(bf16[512,1536]{1,0:T(8,128)(2,1)} %bitcast.8, bf16[12288,1536]{1,0:T(8,128)(2,1)} %bitcast.6, bf16[1536,128]{1,0:T(8,128)(2,1)} %w.1, ...), custom_call_target="tpu_custom_call" | custom-call | tf_op jit(solution)/shard_map/project/pallas_call | solution.py:336
  16.7 0.0 copy-done
  16.7 10.0 %tail.1.p_ext = bf16[12288,256]{1,0:T(8,128)(2,1)S(1)} custom-call(s32[8,256]{1,0:T(8,128)S(1)} %get-tuple-element.9.table, bf16[12288,1536]{1,0:T(8,128)(2,1)} %bitcast.7, bf16[1536,128]{1,0:T(8,128)(2,1)S(1)} %copy-done, bf16[768,128]{1,0:T(8,128)(2,1)S(1)} %get-tuple-element.11.nmt, ...), custom_call_target="tpu_custom_call", output_to_operand_aliasing={{}: (4, {})} | custom-call | tf_op jit(solution)/shard_map/tail/pallas_call | solution.py:360
  26.8 19.3 %score.1.best = f32[16,16,256]{2,1,0:T(8,128)S(1)} custom-call(s32[8,256]{1,0:T(8,128)S(1)} %get-tuple-element.9.table, bf16[4096,128]{1,0:T(8,128)(2,1)S(1)} %get-tuple-element.10.q_all, bf16[12288,256]{1,0:T(8,128)(2,1)S(1)} %tail.1.p_ext), custom_call_target="tpu_custom_call" | custom-call | tf_op jit(solution)/shard_map/score/pallas_call | solution.py:371
  46.7 5.4 %gather.1.scores = f32[128,128]{1,0:T(8,128)S(1)} custom-call(f32[1]{0:T(128)} %bitcast.5.temp, f32[16,16,256]{2,1,0:T(8,128)S(1)} %score.1.best, bf16[4096,128]{1,0:T(8,128)(2,1)S(1)} %get-tuple-element.13.seg), custom_call_target="tpu_custom_call" | custom-call | tf_op jit(solution)/shard_map/gather/pallas_call | solution.py:385
  52.1 0.7 %loss.1 = (f32[1,16]{1,0:T(1,128)}, f32[1,1]{1,0:T(1,128)}) custom-call(f32[128,128]{1,0:T(8,128)S(1)} %gather.1.scores), custom_call_target="tpu_custom_call" | custom-call | tf_op jit(solution)/shard_map/loss/pallas_call | solution.py:395
Async XLA Ops:
  0.6 16.1 %copy-start = (bf16[1536,128]{1,0:T(8,128)(2,1)S(1)}, bf16[1536,128]{1,0:T(8,128)(2,1)}, u32[]{:S(2)}) copy-start(bf16[1536,128]{1,0:T(8,128)(2,1)} %w.1) | copy-start | bytes 1179652

commit v4 on v3

--- a/solution.py
+++ b/solution.py
@@ -12,8 +12,8 @@
 BIG = 1e30
 UNIT = 64
 LANES = 8
-RING = 4
-HEAD = 256
+RING = 3
+HEAD = 448
 GROUP = 4
 TAIL_RING = 8
 
@@ -136,7 +136,8 @@
 
         return carry
 
-    lax.fori_loop(0, nd, project, 0)
+    cut1, cut2 = (7 * nd) // 16, (12 * nd) // 16
+    lax.fori_loop(0, cut1, project, 0)
     for rel in (2, 4):
         received(rel)
         send(rel, 1)
@@ -159,8 +160,10 @@
     where = iota((rows * 8, n), 0)
     seg[...] = as_bf((where >= first) & (where < end))
 
+    lax.fori_loop(cut1, cut2, project, 0)
     received(6)
     send(6, 1)
+    lax.fori_loop(cut2, nd, project, 0)
     for rel in (1, 3, 5, 7):
         received(rel)
     for copy in mask_sent + sent:
@@ -178,8 +181,8 @@
     for g in range(TAIL_RING):
         @pl.when(g < steps)
         def _():
-            for copy in copies(g):
-                copy.start()
+            for k, copy in enumerate(copies(g)):
+                copy.start(priority=k % 2)
 
     def step(g, carry):
         for copy in copies(g):
@@ -193,8 +196,8 @@
 
         @pl.when(g + TAIL_RING < steps)
         def _():
-            for copy in copies(g + TAIL_RING):
-                copy.start()
+            for k, copy in enumerate(copies(g + TAIL_RING)):
+                copy.start(priority=k % 2)
 
         return carry
 

time: 52.6 us -> 54.4 us (1.034); the launches traced: 52.8 us -> 54 us
  Pallas kernels: 51.4 us -> 52.7 us
    pallas_call x1, Pallas kernels: 10 us -> 7.28 us  [local_step(): pl.pallas_call(functools.partial(tail_kernel, dlen // UNIT), out_shape=pl...]
    pallas_call x1, Pallas kernels: 16.1 us -> 18.5 us  [local_step(): pl.pallas_call(functools.partial(project_kernel, nq, qlen, nd, dlen), out...]
    pallas_call x1, Pallas kernels: 19.3 us -> 21.4 us  [local_step(): pl.pallas_call(functools.partial(score_kernel, nd, rows, tiles), out_shap...]
    pallas_call x1, Pallas kernels: 5.37 us -> 4.73 us  [local_step(): pl.pallas_call(functools.partial(gather_kernel, nd, tiles), out_shape=plt...]
where the time goes in v4:
time: 54.4 us; the launch traced here: 54 us
  Pallas kernels  52.7 us (97%)
  between operations  1.33 us (2%)
    pallas_call x1, Pallas kernels, local_step(): pl.pallas_call(functools.partial(score_kernel, nd, rows, tiles), out_shap...  21.4 us
    pallas_call x1, Pallas kernels, local_step(): pl.pallas_call(functools.partial(project_kernel, nq, qlen, nd, dlen), out...  18.5 us
    pallas_call x1, Pallas kernels, local_step(): pl.pallas_call(functools.partial(tail_kernel, dlen // UNIT), out_shape=pl...  7.28 us
    pallas_call x1, Pallas kernels, local_step(): pl.pallas_call(functools.partial(gather_kernel, nd, tiles), out_shape=plt...  4.73 us

profile of v4, /device:TPU:0, one launch (start us, length us, event | category | flops | bytes accessed | tf_op | source)
XLA Modules:
  0.0 54.0 jit_solution(16898385155712096054)
XLA Ops:
  0.6 0.0 copy-start
  0.6 18.5 %project.1 = (bf16[4096,128]{1,0:T(8,128)(2,1)S(1)}, bf16[12288,256]{1,0:T(8,128)(2,1)S(1)}, s32[8,256]{1,0:T(8,128)S(1)}, bf16[4096,128]{1,0:T(8,128)(2,1)S(1)}, bf16[768,128]{1,0:T(8,128)(2,1)S(1)}) custom-call(bf16[512,1536]{1,0:T(8,128)(2,1)} %bitcast.8, bf16[12288,1536]{1,0:T(8,128)(2,1)} %bitcast.6, bf16[1536,128]{1,0:T(8,128)(2,1)} %w.1, ...), custom_call_target="tpu_custom_call" | custom-call | tf_op jit(solution)/shard_map/project/pallas_call | solution.py:339
  19.2 0.0 copy-done
  19.2 7.3 %tail.1.p_ext = bf16[12288,256]{1,0:T(8,128)(2,1)S(1)} custom-call(s32[8,256]{1,0:T(8,128)S(1)} %get-tuple-element.9.table, bf16[12288,1536]{1,0:T(8,128)(2,1)} %bitcast.7, bf16[1536,128]{1,0:T(8,128)(2,1)S(1)} %copy-done, bf16[768,128]{1,0:T(8,128)(2,1)S(1)} %get-tuple-element.11.nmt, ...), custom_call_target="tpu_custom_call", output_to_operand_aliasing={{}: (4, {})} | custom-call | tf_op jit(solution)/shard_map/tail/pallas_call | solution.py:363
  26.5 21.4 %score.1.best = f32[16,16,256]{2,1,0:T(8,128)S(1)} custom-call(s32[8,256]{1,0:T(8,128)S(1)} %get-tuple-element.9.table, bf16[4096,128]{1,0:T(8,128)(2,1)S(1)} %get-tuple-element.10.q_all, bf16[12288,256]{1,0:T(8,128)(2,1)S(1)} %tail.1.p_ext), custom_call_target="tpu_custom_call" | custom-call | tf_op jit(solution)/shard_map/score/pallas_call | solution.py:374
  48.6 4.7 %gather.1.scores = f32[128,128]{1,0:T(8,128)S(1)} custom-call(f32[1]{0:T(128)} %bitcast.5.temp, f32[16,16,256]{2,1,0:T(8,128)S(1)} %score.1.best, bf16[4096,128]{1,0:T(8,128)(2,1)S(1)} %get-tuple-element.13.seg), custom_call_target="tpu_custom_call" | custom-call | tf_op jit(solution)/shard_map/gather/pallas_call | solution.py:388
  53.3 0.7 %loss.1 = (f32[1,16]{1,0:T(1,128)}, f32[1,1]{1,0:T(1,128)}) custom-call(f32[128,128]{1,0:T(8,128)S(1)} %gather.1.scores), custom_call_target="tpu_custom_call" | custom-call | tf_op jit(solution)/shard_map/loss/pallas_call | solution.py:398
Async XLA Ops:
  0.6 18.6 %copy-start = (bf16[1536,128]{1,0:T(8,128)(2,1)S(1)}, bf16[1536,128]{1,0:T(8,128)(2,1)}, u32[]{:S(2)}) copy-start(bf16[1536,128]{1,0:T(8,128)(2,1)} %w.1) | copy-start | bytes 1179652

commit v5 on v3

--- a/solution.py
+++ b/solution.py
@@ -14,8 +14,7 @@
 LANES = 8
 RING = 4
 HEAD = 256
-GROUP = 4
-TAIL_RING = 8
+GROUP = 16
 
 
 def iota(shape, dim):
@@ -106,29 +105,29 @@
     off = jnp.concatenate([1.0 - dmask.astype(F32), jnp.zeros((128 - nd, dlen), F32)], axis=0)
     nmt[...] = jnp.transpose(off).astype(BF16)
     last = jnp.max(dmask * (iota((nd, dlen), 1) + 1), axis=1, keepdims=True).astype(F32)
-    per_doc = dlen // UNIT
     count = jnp.floor((last + (UNIT - 1.0)) * (1.0 / UNIT))
     sums = as_bf(iota((nd, nd), 0) >= iota((nd, nd), 1))
 
-    def listing(at, count, first):
+    def listing(at, count, per, first):
         upto = dot(sums, jnp.broadcast_to(count, (nd, 128)).astype(BF16))[:, 0:1]
         total = jnp.max(upto, axis=0, keepdims=True)
         slot_id = jnp.minimum(iota((nd, 256), 1).astype(F32), jnp.maximum(total - 1.0, 0.0))
         passed = slot_id >= upto
-        unit = slot_id[0:1] + first + jnp.sum(jnp.where(passed, per_doc - count, 0.0), axis=0, keepdims=True)
+        unit = slot_id[0:1] + first + jnp.sum(jnp.where(passed, per - count, 0.0), axis=0, keepdims=True)
         doc = jnp.sum(jnp.where(passed, 1.0, 0.0), axis=0, keepdims=True)
         table[at:at + 1, :] = unit.astype(jnp.int32)
         table[at + 1:at + 2, :] = doc.astype(jnp.int32)
         table[at + 2:at + 3, :] = jnp.broadcast_to(total, (1, 256)).astype(jnp.int32)
 
-    listing(0, count, 0.0)
-    listing(4, jnp.maximum(count - HEAD // UNIT, 0.0), float(HEAD // UNIT))
+    head = float(HEAD // UNIT)
+    listing(0, jnp.minimum(count, head), head, 0.0)
+    listing(4, jnp.maximum(count - head, 0.0), float(dlen // UNIT), head)
 
     def project(j, carry):
         slot = lax.rem(j, RING)
         doc_copy(j, slot).wait()
-        p_ext[pl.ds(j * dlen, HEAD), 0:128] = unit_rows(dot(d_buf[slot], w_buf[...]))
-        p_ext[pl.ds(j * dlen, HEAD), 128:256] = mask_features(j, nmt[0:HEAD, :])
+        p_ext[pl.ds(j * HEAD, HEAD), 0:128] = unit_rows(dot(d_buf[slot], w_buf[...]))
+        p_ext[pl.ds(j * HEAD, HEAD), 128:256] = mask_features(j, nmt[0:HEAD, :])
 
         @pl.when(j + RING < nd)
         def _():
@@ -136,10 +135,12 @@
 
         return carry
 
-    lax.fori_loop(0, nd, project, 0)
+    cut = (13 * nd) // 16
+    lax.fori_loop(0, cut, project, 0)
     for rel in (2, 4):
         received(rel)
         send(rel, 1)
+    lax.fori_loop(cut, nd, project, 0)
 
     for rel in range(1, 8):
         remote(qm_all, nq, rel, rel, ms_sem.at[rel - 1], mr_sem.at[rel - 1]).wait_recv()
@@ -167,48 +168,26 @@
         copy.wait_send()
 
 
-def tail_kernel(per_doc, table, d_hbm, w, nmt, p_head, p_ext, d_buf, sem):
-    steps = (table[6, 0] + (GROUP - 1)) // GROUP
-
-    def copies(g):
-        slot = lax.rem(g, TAIL_RING)
-        return [pltpu.make_async_copy(d_hbm.at[pl.ds(pl.multiple_of(table[4, g * GROUP + k] * UNIT, UNIT), UNIT)],
-                                      d_buf.at[slot, pl.ds(k * UNIT, UNIT)], sem.at[slot]) for k in range(GROUP)]
-
-    for g in range(TAIL_RING):
-        @pl.when(g < steps)
-        def _():
-            for copy in copies(g):
-                copy.start()
-
-    def step(g, carry):
-        for copy in copies(g):
-            copy.wait()
-        value = unit_rows(dot(d_buf[lax.rem(g, TAIL_RING)], w[...]))
+def score_body(nd, rows, tiles, per_doc, hidden, table, q_all, p_head, nmt, w, d_hbm, out, q_list, best, p_tail, d_buf,
+               sem, accs):
+    n_head, n_tail = table[2, 0], table[6, 0]
+    n_group = (n_tail + (GROUP - 1)) // GROUP
+
+    def fetch(g, carry):
         for k in range(GROUP):
-            unit, doc = table[4, g * GROUP + k], table[5, g * GROUP + k]
-            at = pl.ds(pl.multiple_of(unit * UNIT, UNIT), UNIT)
-            p_ext[at, 0:128] = value[k * UNIT:(k + 1) * UNIT]
-            p_ext[at, 128:256] = mask_features(doc, nmt[pl.ds(pl.multiple_of((unit - doc * per_doc) * UNIT, UNIT), UNIT), :])
-
-        @pl.when(g + TAIL_RING < steps)
-        def _():
-            for copy in copies(g + TAIL_RING):
-                copy.start()
-
+            row = pl.multiple_of(table[4, g * GROUP + k] * UNIT, UNIT)
+            pltpu.make_async_copy(d_hbm.at[pl.ds(row, UNIT)], d_buf.at[g, pl.ds(k * UNIT, UNIT)],
+                                  sem.at[g]).start(priority=k % 2)
         return carry
 
-    lax.fori_loop(0, steps, step, 0)
-
-
-def score_body(nd, rows, tiles, table, q_all, p_ext, out, q_list, best, accs):
+    lax.fori_loop(0, n_group, fetch, 0)
+
     floor = jnp.full((nd, 8, 256), -3e38, F32)
     out[...] = jnp.zeros_like(out)
     for dev in range(8):
         q_list[pl.ds(pl.multiple_of(table[3, dev], 16), rows), :] = q_all[dev * rows:(dev + 1) * rows, :]
     q_list[pl.ds(pl.multiple_of(table[3, 7], 16) + rows, 256), :] = jnp.zeros((256, 128), BF16)
     n_tile = (table[3, 8] + 255) // 256
-    n_trip = (table[2, 0] + (2 * LANES - 1)) // (2 * LANES)
     away = jnp.full((256, 128), -BIG, BF16)
 
     def push(tile):
@@ -217,60 +196,113 @@
         for unit in range(2):
             pltpu.matmul_push_rhs(rhs, staging_register=0, mxu_index=unit, transpose=True)
 
-    def drain(unit, k, slot, trip):
-        value = pltpu.matmul_pop(accs[unit][k])
-        top = value[0:8]
-        for r in range(1, UNIT // 8):
-            top = jnp.maximum(top, value[8 * r:8 * r + 8])
-        doc = table[1, trip * (2 * LANES) + 2 * k + unit]
-        best[unit][slot, doc] = jnp.maximum(best[unit][slot, doc], top)
-
-    def step(slot, trip, prev_slot, prev_trip, first):
+    def unstage():
+        for unit in range(2):
+            pltpu.matmul_acc_lhs(accs[unit][0], jnp.zeros((UNIT, 256), BF16), load_staged_rhs=0)
+            pltpu.matmul_pop(accs[unit][0])
+
+    def finish(slot, tile):
+        out[tile] = jnp.max(jnp.maximum(best[0][slot], best[1][slot]), axis=1)
+
+    def sweep(at, count, row_of, src, is_last):
+        n_trip = (count + (2 * LANES - 1)) // (2 * LANES)
+        todo = jnp.where(count > 0, n_tile, 0)
+
+        def drain(unit, k, slot, trip):
+            value = pltpu.matmul_pop(accs[unit][k])
+            top = value[0:8]
+            for r in range(1, UNIT // 8):
+                top = jnp.maximum(top, value[8 * r:8 * r + 8])
+            doc = table[at + 1, jnp.maximum(trip, 0) * (2 * LANES) + 2 * k + unit]
+            best[unit][slot, doc] = jnp.maximum(best[unit][slot, doc], top)
+
+        def step(slot, trip, prev_slot, prev_trip, first):
+            for k in range(LANES):
+                for unit in range(2):
+                    drain(unit, k, prev_slot, prev_trip)
+                    row = row_of(trip * (2 * LANES) + 2 * k + unit) * UNIT
+                    lhs = src[pl.ds(pl.multiple_of(row, UNIT), UNIT), :]
+                    pltpu.matmul_acc_lhs(accs[unit][k], lhs, load_staged_rhs=0 if first and k == 0 else None)
+
+        push(0)
+
+        def per_tile(tile, carry):
+            if not is_last:
+                best[0][tile + 1] = floor
+                best[1][tile + 1] = floor
+            step(tile + 1, 0, tile, n_trip - 1, True)
+            if is_last:
+                finish(tile, jnp.maximum(tile - 1, 0))
+            push(jnp.minimum(tile + 1, tiles - 1))
+
+            def per_trip(trip, carry):
+                step(tile + 1, trip, tile + 1, trip - 1, False)
+                return carry
+
+            lax.fori_loop(1, n_trip, per_trip, 0)
+            return carry
+
+        lax.fori_loop(0, todo, per_tile, 0)
         for k in range(LANES):
             for unit in range(2):
-                drain(unit, k, prev_slot, prev_trip)
-                row = table[0, trip * (2 * LANES) + 2 * k + unit] * UNIT
-                lhs = p_ext[pl.ds(pl.multiple_of(row, UNIT), UNIT), :]
-                pltpu.matmul_acc_lhs(accs[unit][k], lhs, load_staged_rhs=0 if first and k == 0 else None)
-
-    def finish(slot, tile):
-        both = jnp.maximum(best[0][slot], best[1][slot])
-        out[tile] = jnp.max(both, axis=1)
+                drain(unit, k, todo, n_trip - 1)
+        unstage()
 
     for unit in range(2):
+        best[unit][0] = floor
         for k in range(LANES):
             pltpu.matmul_pop(accs[unit][k])
-    push(0)
-
-    def per_tile(tile, carry):
-        best[0][tile + 1] = floor
-        best[1][tile + 1] = floor
-        step(tile + 1, 0, tile, n_trip - 1, True)
-        finish(tile, jnp.maximum(tile - 1, 0))
-        push(jnp.minimum(tile + 1, tiles - 1))
-
-        def per_trip(trip, carry):
-            step(tile + 1, trip, tile + 1, trip - 1, False)
-            return carry
-
-        lax.fori_loop(1, n_trip, per_trip, 0)
+    sweep(0, n_head, lambda i: table[0, i], p_head, False)
+
+    depth = hidden // 256
+    blank = jnp.zeros((256, 128), BF16)
+
+    def push_w(k):
+        rhs = jnp.concatenate([w[k * 256:(k + 1) * 256, :], blank], axis=1)
+        for unit in range(2):
+            pltpu.matmul_push_rhs(rhs, staging_register=0, mxu_index=unit, transpose=False)
+
+    push_w(0)
+
+    def project(g, carry):
+        pltpu.make_async_copy(d_hbm.at[pl.ds(0, GROUP * UNIT)], d_buf.at[g], sem.at[g]).wait()
+        for half in range(2):
+            for k in range(depth):
+                for q in range(4):
+                    for unit in range(2):
+                        at = (half * 8 + unit * 4 + q) * UNIT
+                        pltpu.matmul_acc_lhs(accs[unit][half * 4 + q],
+                                             d_buf[g, at:at + UNIT, k * 256:(k + 1) * 256],
+                                             load_staged_rhs=0 if q == 0 else None)
+                push_w((k + 1) % depth)
+            for q in range(4):
+                for unit in range(2):
+                    index = g * GROUP + half * 8 + unit * 4 + q
+                    value = pltpu.matmul_pop(accs[unit][half * 4 + q])[:, 0:128]
+                    dst = pl.ds(pl.multiple_of(index * UNIT, UNIT), UNIT)
+                    doc = table[5, index]
+                    off = nmt[pl.ds(pl.multiple_of((table[4, index] - doc * per_doc) * UNIT, UNIT), UNIT), :]
+                    p_tail[dst, 0:128] = unit_rows(value)
+                    p_tail[dst, 128:256] = mask_features(doc, off)
         return carry
 
-    best[0][0] = floor
-    best[1][0] = floor
-    lax.fori_loop(0, n_tile, per_tile, 0)
-    for k in range(LANES):
-        for unit in range(2):
-            drain(unit, k, n_tile, n_trip - 1)
-    finish(n_tile, n_tile - 1)
-    for unit in range(2):
-        pltpu.matmul_acc_lhs(accs[unit][0], jnp.zeros((UNIT, 256), BF16), load_staged_rhs=0)
-        pltpu.matmul_pop(accs[unit][0])
-
-
-def score_kernel(nd, rows, tiles, table, q_all, p_ext, out, q_list, best0, best1):
+    lax.fori_loop(0, n_group, project, 0)
+    unstage()
+
+    sweep(4, n_tail, lambda i: jnp.minimum(i, n_tail - 1), p_tail, True)
+
+    def finish_all(tile, carry):
+        finish(tile + 1, tile)
+        return carry
+
+    lax.fori_loop(jnp.where(n_tail > 0, n_tile - 1, 0), n_tile, finish_all, 0)
+
+
+def score_kernel(nd, rows, tiles, per_doc, hidden, table, q_all, p_head, nmt, w, d_hbm, out, q_list, best0, best1, p_tail,
+                 d_buf, sem):
     def body(*accs):
-        score_body(nd, rows, tiles, table, q_all, p_ext, out, q_list, (best0, best1), (accs[:LANES], accs[LANES:]))
+        score_body(nd, rows, tiles, per_doc, hidden, table, q_all, p_head, nmt, w, d_hbm, out, q_list, (best0, best1),
+                   p_tail, d_buf, sem, (accs[:LANES], accs[LANES:]))
 
     pl.run_scoped(body, *[pltpu.ACC(0)((UNIT, 256), F32)] * LANES, *[pltpu.ACC(1)((UNIT, 256), F32)] * LANES)
 
@@ -337,7 +369,7 @@
             functools.partial(project_kernel, nq, qlen, nd, dlen),
             out_shape=[
                 pltpu.VMEM((rows * 8, 128), BF16),
-                pltpu.VMEM((nd * dlen, 256), BF16),
+                pltpu.VMEM((nd * HEAD, 256), BF16),
                 pltpu.VMEM((8, 256), jnp.int32),
                 pltpu.VMEM((rows * 8, nq * 8), BF16),
                 pltpu.VMEM((dlen, 128), BF16),
@@ -357,30 +389,24 @@
         )(hbm(query_hidden.reshape(rows, hidden)), hbm(doc_hidden.reshape(nd * dlen, hidden)), hbm(w_proj),
           hbm(query_mask), hbm(doc_mask))
 
-        p_ext = pl.pallas_call(
-            functools.partial(tail_kernel, dlen // UNIT),
-            out_shape=pltpu.VMEM((nd * dlen, 256), BF16),
-            in_specs=[SMEM, ANY, VMEM, VMEM, VMEM],
-            out_specs=VMEM,
-            scratch_shapes=[pltpu.VMEM((TAIL_RING, GROUP * UNIT, hidden), BF16), DMA((TAIL_RING,))],
-            input_output_aliases={4: 0},
-            compiler_params=pltpu.CompilerParams(vmem_limit_bytes=30 * 2**20),
-            name='tail',
-        )(table, hbm(doc_hidden.reshape(nd * dlen, hidden)), w_proj, vmem(nmt), vmem(p_head))
-
+        tail_rows = nd * (dlen - HEAD)
+        groups = tail_rows // (GROUP * UNIT)
         best = pl.pallas_call(
-            functools.partial(score_kernel, nd, rows, tiles),
+            functools.partial(score_kernel, nd, rows, tiles, dlen // UNIT, hidden),
             out_shape=pltpu.VMEM((tiles, nd, 256), F32),
-            in_specs=[SMEM, VMEM, VMEM],
+            in_specs=[SMEM, VMEM, VMEM, VMEM, VMEM, ANY],
             out_specs=VMEM,
             scratch_shapes=[
                 pltpu.VMEM((rows * 8 + 512, 128), BF16),
                 pltpu.VMEM((tiles + 1, nd, 8, 256), F32),
                 pltpu.VMEM((tiles + 1, nd, 8, 256), F32),
+                pltpu.VMEM((tail_rows, 256), BF16),
+                pltpu.VMEM((groups, GROUP * UNIT, hidden), BF16),
+                DMA((groups,)),
             ],
-            compiler_params=pltpu.CompilerParams(vmem_limit_bytes=30 * 2**20),
+            compiler_params=pltpu.CompilerParams(vmem_limit_bytes=50 * 2**20),
             name='score',
-        )(table, vmem(q_all), vmem(p_ext))
+        )(table, vmem(q_all), vmem(p_head), vmem(nmt), w_proj, hbm(doc_hidden.reshape(nd * dlen, hidden)))
 
         scores = pl.pallas_call(
             functools.partial(gather_kernel, nd, tiles),

time: 52.6 us -> 48.1 us (0.914); the launches traced: 52.8 us -> 47.6 us
  Pallas kernels: 51.4 us -> 46.3 us
    pallas_call x2 -> x1, Pallas kernels: 29.3 us -> 23.7 us  [local_step(): pl.pallas_call(functools.partial(score_kernel, nd, rows, tiles, dlen // U...]
where the time goes in v5:
time: 48.1 us; the launch traced here: 47.6 us
  Pallas kernels  46.3 us (96%)
  between operations  1.32 us (3%)
    pallas_call x1, Pallas kernels, local_step(): pl.pallas_call(functools.partial(score_kernel, nd, rows, tiles, dlen // U...  23.7 us
    pallas_call x1, Pallas kernels, local_step(): pl.pallas_call(functools.partial(project_kernel, nq, qlen, nd, dlen), out...  16.1 us
    pallas_call x1, Pallas kernels, local_step(): pl.pallas_call(functools.partial(gather_kernel, nd, tiles), out_shape=plt...  5.75 us

profile of v5, /device:TPU:0, one launch (start us, length us, event | category | flops | bytes accessed | tf_op | source)
XLA Modules:
  0.0 47.6 jit_solution(16613078295668657620)
XLA Ops:
  0.6 0.0 copy-start
  0.6 16.1 %project.1 = (bf16[4096,128]{1,0:T(8,128)(2,1)S(1)}, bf16[4096,256]{1,0:T(8,128)(2,1)S(1)}, s32[8,256]{1,0:T(8,128)S(1)}, bf16[4096,128]{1,0:T(8,128)(2,1)S(1)}, bf16[768,128]{1,0:T(8,128)(2,1)S(1)}) custom-call(bf16[512,1536]{1,0:T(8,128)(2,1)} %bitcast.8, bf16[12288,1536]{1,0:T(8,128)(2,1)} %bitcast.6, bf16[1536,128]{1,0:T(8,128)(2,1)} %w.1, ...), custom_call_target="tpu_custom_call" | custom-call | tf_op jit(solution)/shard_map/project/pallas_call | solution.py:368
  16.7 0.0 copy-done
  16.8 23.7 %score.1.best = f32[16,16,256]{2,1,0:T(8,128)S(1)} custom-call(s32[8,256]{1,0:T(8,128)S(1)} %get-tuple-element.9.table, bf16[4096,128]{1,0:T(8,128)(2,1)S(1)} %get-tuple-element.10.q_all, bf16[4096,256]{1,0:T(8,128)(2,1)S(1)} %get-tuple-element.11.p_head, bf16[768,128]{1,0:T(8,128)(2,1)S(1)} %get-tuple-element.12.nmt, bf16[1536,128]{1,0:T(8,128)(2,1)S(1)} %copy-done, ...), custom_call_target="tpu_custom_call" | custom-call | tf_op jit(solution)/shard_map/score/pallas_call | solution.py:394
  41.2 5.8 %gather.1.scores = f32[128,128]{1,0:T(8,128)S(1)} custom-call(f32[1]{0:T(128)} %bitcast.5.temp, f32[16,16,256]{2,1,0:T(8,128)S(1)} %score.1.best, bf16[4096,128]{1,0:T(8,128)(2,1)S(1)} %get-tuple-element.13.seg), custom_call_target="tpu_custom_call" | custom-call | tf_op jit(solution)/shard_map/gather/pallas_call | solution.py:411
  46.9 0.7 %loss.1 = (f32[1,16]{1,0:T(1,128)}, f32[1,1]{1,0:T(1,128)}) custom-call(f32[128,128]{1,0:T(8,128)S(1)} %gather.1.scores), custom_call_target="tpu_custom_call" | custom-call | tf_op jit(solution)/shard_map/loss/pallas_call | solution.py:421
Async XLA Ops:
  0.6 16.1 %copy-start = (bf16[1536,128]{1,0:T(8,128)(2,1)S(1)}, bf16[1536,128]{1,0:T(8,128)(2,1)}, u32[]{:S(2)}) copy-start(bf16[1536,128]{1,0:T(8,128)(2,1)} %w.1) | copy-start | bytes 1179652

commit v6 on v5

--- a/solution.py
+++ b/solution.py
@@ -13,7 +13,7 @@
 UNIT = 64
 LANES = 8
 RING = 4
-HEAD = 256
+HEAD = 320
 GROUP = 16
 
 
@@ -43,8 +43,8 @@
     return jnp.where(iota(off.shape, 1) == doc, off.astype(F32), 0.0).astype(BF16)
 
 
-def project_kernel(nq, qlen, nd, dlen, q_hbm, d_hbm, w_hbm, qm_hbm, dm_hbm, q_all, p_ext, table, seg, nmt,
-                   qm_all, q_buf, w_buf, dm_buf, d_buf, in_sem, d_sem, qs_sem, qr_sem, ms_sem, mr_sem):
+def project_kernel(nq, qlen, nd, dlen, q_hbm, d_hbm, w_hbm, qm_hbm, dm_hbm, q_all, p_ext, table, seg, nmt, w_buf,
+                   qm_all, q_buf, dm_buf, d_buf, in_sem, d_sem, qs_sem, qr_sem, ms_sem, mr_sem):
     rows = nq * qlen
     n = nq * 8
     me = place(0)[1]
@@ -57,9 +57,6 @@
     def doc_copy(j, slot):
         return pltpu.make_async_copy(d_hbm.at[pl.ds(j * dlen, HEAD)], d_buf.at[slot], d_sem.at[slot])
 
-    for j in range(RING):
-        doc_copy(j, j).start()
-
     barrier = pltpu.get_barrier_semaphore()
     for rel in range(1, 8):
         pl.semaphore_signal(barrier, inc=1, device_id=place(rel)[0], device_id_type=MESH)
@@ -99,6 +96,8 @@
 
     for rel in (2, 4, 6, 1):
         send(0, rel)
+    for j in range(RING):
+        doc_copy(j, j).start()
 
     ins[1].wait()
     dmask = dm_buf[...]
@@ -135,12 +134,11 @@
 
         return carry
 
-    cut = (13 * nd) // 16
-    lax.fori_loop(0, cut, project, 0)
+    cut1, cut2 = (8 * nd) // 16, (14 * nd) // 16
+    lax.fori_loop(0, cut1, project, 0)
     for rel in (2, 4):
         received(rel)
         send(rel, 1)
-    lax.fori_loop(cut, nd, project, 0)
 
     for rel in range(1, 8):
         remote(qm_all, nq, rel, rel, ms_sem.at[rel - 1], mr_sem.at[rel - 1]).wait_recv()
@@ -149,10 +147,13 @@
     counts = lax.dot_general(jnp.ones((16, qlen), BF16), every, (((1,), (1,)), ((), ())), preferred_element_type=F32)
     counts_bf = counts.astype(BF16)
     in_dev = dot(counts_bf, as_bf((row // nq == col // nq) & (row < col)))
-    padded = jnp.floor((dot(counts_bf, as_bf(row // nq == col // nq)) + 15.0) * (1.0 / 16.0)) * 16.0
-    padded_bf = padded.astype(BF16)
-    begin = dot(padded_bf, as_bf((row // nq < col // nq) & (row % nq == 0))) + in_dev
-    starts = dot(padded_bf, as_bf((row // nq < col) & (row % nq == 0)))
+    valid = dot(counts_bf, as_bf(row // nq == col // nq))
+    high = jnp.floor(valid * (1.0 / 16.0))
+    low = (valid - high * 16.0).astype(BF16)
+    high = high.astype(BF16)
+    total_of = lambda cond: dot(high, as_bf(cond)) * 16.0 + dot(low, as_bf(cond))
+    begin = total_of((row // nq < col // nq) & (row % nq == 0)) + in_dev
+    starts = total_of((row // nq < col) & (row % nq == 0))
     table[3:4, 0:128] = starts[0:1].astype(jnp.int32)
     table[3:4, 128:256] = starts[0:1].astype(jnp.int32)
     first = begin[0:1].astype(jnp.int32)
@@ -160,8 +161,10 @@
     where = iota((rows * 8, n), 0)
     seg[...] = as_bf((where >= first) & (where < end))
 
+    lax.fori_loop(cut1, cut2, project, 0)
     received(6)
     send(6, 1)
+    lax.fori_loop(cut2, nd, project, 0)
     for rel in (1, 3, 5, 7):
         received(rel)
     for copy in mask_sent + sent:
@@ -185,13 +188,13 @@
     floor = jnp.full((nd, 8, 256), -3e38, F32)
     out[...] = jnp.zeros_like(out)
     for dev in range(8):
-        q_list[pl.ds(pl.multiple_of(table[3, dev], 16), rows), :] = q_all[dev * rows:(dev + 1) * rows, :]
-    q_list[pl.ds(pl.multiple_of(table[3, 7], 16) + rows, 256), :] = jnp.zeros((256, 128), BF16)
+        q_list[pl.ds(table[3, dev], rows), :] = q_all[dev * rows:(dev + 1) * rows, :].astype(F32)
+    q_list[pl.ds(table[3, 7] + rows, 256), :] = jnp.zeros((256, 128), F32)
     n_tile = (table[3, 8] + 255) // 256
     away = jnp.full((256, 128), -BIG, BF16)
 
     def push(tile):
-        q_tile = q_list[pl.ds(pl.multiple_of(tile * 256, 256), 256), :]
+        q_tile = q_list[pl.ds(pl.multiple_of(tile * 256, 256), 256), :].astype(BF16)
         rhs = jnp.concatenate([q_tile, away], axis=1)
         for unit in range(2):
             pltpu.matmul_push_rhs(rhs, staging_register=0, mxu_index=unit, transpose=True)
@@ -365,7 +368,7 @@
         tiles = rows * 8 // 256
         hbm = lambda x: pltpu.with_memory_space_constraint(x, pltpu.HBM)
         vmem = lambda x: pltpu.with_memory_space_constraint(x, pltpu.VMEM)
-        q_all, p_head, table, seg, nmt = pl.pallas_call(
+        q_all, p_head, table, seg, nmt, w_vmem = pl.pallas_call(
             functools.partial(project_kernel, nq, qlen, nd, dlen),
             out_shape=[
                 pltpu.VMEM((rows * 8, 128), BF16),
@@ -373,13 +376,13 @@
                 pltpu.VMEM((8, 256), jnp.int32),
                 pltpu.VMEM((rows * 8, nq * 8), BF16),
                 pltpu.VMEM((dlen, 128), BF16),
+                pltpu.VMEM((hidden, 128), BF16),
             ],
             in_specs=[ANY] * 5,
-            out_specs=[VMEM] * 5,
+            out_specs=[VMEM] * 6,
             scratch_shapes=[
                 pltpu.VMEM((nq * 8, qlen), jnp.int32),
                 pltpu.VMEM((rows, hidden), BF16),
-                pltpu.VMEM((hidden, 128), BF16),
                 pltpu.VMEM((nd, dlen), jnp.int32),
                 pltpu.VMEM((RING, HEAD, hidden), BF16),
                 DMA((4,)), DMA((RING,)), DMA((7,)), DMA((7,)), DMA((7,)), DMA((7,)),
@@ -397,7 +400,7 @@
             in_specs=[SMEM, VMEM, VMEM, VMEM, VMEM, ANY],
             out_specs=VMEM,
             scratch_shapes=[
-                pltpu.VMEM((rows * 8 + 512, 128), BF16),
+                pltpu.VMEM((rows * 8 + 512, 128), F32),
                 pltpu.VMEM((tiles + 1, nd, 8, 256), F32),
                 pltpu.VMEM((tiles + 1, nd, 8, 256), F32),
                 pltpu.VMEM((tail_rows, 256), BF16),
@@ -406,7 +409,7 @@
             ],
             compiler_params=pltpu.CompilerParams(vmem_limit_bytes=50 * 2**20),
             name='score',
-        )(table, vmem(q_all), vmem(p_head), vmem(nmt), w_proj, hbm(doc_hidden.reshape(nd * dlen, hidden)))
+        )(table, vmem(q_all), vmem(p_head), vmem(nmt), vmem(w_vmem), hbm(doc_hidden.reshape(nd * dlen, hidden)))
 
         scores = pl.pallas_call(
             functools.partial(gather_kernel, nd, tiles),

time: 48.1 us -> 49.7 us (1.033); the launches traced: 47.6 us -> 50.6 us
  Pallas kernels: 46.3 us -> 48.7 us
  local copies, waits for them, and re-layouts: 0.01 us -> 0.59 us
    pallas_call x1, Pallas kernels: 16.1 us -> 17 us  [local_step(): pl.pallas_call(functools.partial(project_kernel, nq, qlen, nd, dlen), out...]
    pallas_call x1, Pallas kernels: 5.75 us -> 6.62 us  [local_step(): pl.pallas_call(functools.partial(gather_kernel, nd, tiles), out_shape=plt...]
    pallas_call x1, Pallas kernels: 23.7 us -> 24.4 us  [local_step(): pl.pallas_call(functools.partial(score_kernel, nd, rows, tiles, dlen // U...]
    unnamed x2, local copies, waits for them, and re-layouts: 0.01 us -> 0.59 us
where the time goes in v6:
time: 49.7 us; the launch traced here: 50.6 us
  Pallas kernels  48.7 us (98%)
  between operations  1.31 us (3%)
  local copies, waits for them, and re-layouts  0.59 us (1%)
    pallas_call x1, Pallas kernels, local_step(): pl.pallas_call(functools.partial(score_kernel, nd, rows, tiles, dlen // U...  24.4 us
    pallas_call x1, Pallas kernels, local_step(): pl.pallas_call(functools.partial(project_kernel, nq, qlen, nd, dlen), out...  17 us
    pallas_call x1, Pallas kernels, local_step(): pl.pallas_call(functools.partial(gather_kernel, nd, tiles), out_shape=plt...  6.62 us

profile of v6, /device:TPU:0, one launch (start us, length us, event | category | flops | bytes accessed | tf_op | source)
XLA Modules:
  0.0 50.6 jit_solution(12549977708204130310)
XLA Ops:
  0.6 17.0 %project.1 = (bf16[4096,128]{1,0:T(8,128)(2,1)S(1)}, bf16[5120,256]{1,0:T(8,128)(2,1)S(1)}, s32[8,256]{1,0:T(8,128)S(1)}, bf16[4096,128]{1,0:T(8,128)(2,1)S(1)},...) custom-call(bf16[512,1536]{1,0:T(8,128)(2,1)} %bitcast.8, bf16[12288,1536]{1,0:T(8,128)(2,1)} %bitcast.6, ...), custom_call_target="tpu_custom_call" | custom-call | tf_op jit(solution)/shard_map/project/pallas_call | solution.py:371
  17.6 0.0 copy-start
  17.6 0.6 %copy-done = s32[8,256]{1,0:T(8,128)} copy-done((s32[8,256]{1,0:T(8,128)}, s32[8,256]{1,0:T(8,128)S(1)}, u32[]{:S(2)}) %copy-start) | copy-done | bytes 8216
  18.2 24.4 %score.1.best = f32[16,16,256]{2,1,0:T(8,128)S(1)} custom-call(s32[8,256]{1,0:T(8,128)} %copy-done, bf16[4096,128]{1,0:T(8,128)(2,1)S(1)} %get-tuple-element.11.q_all, bf16[5120,256]{1,0:T(8,128)(2,1)S(1)} %get-tuple-element.12.p_head, bf16[768,128]{1,0:T(8,128)(2,1)S(1)} %get-tuple-element.13.nmt, bf16[1536,128]{1,0:T(8,128)(2,1)S(1)} %get-tuple-element.14.w, ...), custom_call_target="tpu_custom_call" | custom-call | tf_op jit(solution)/shard_map/score/pallas_call | solution.py:397
  43.3 6.6 %gather.1.scores = f32[128,128]{1,0:T(8,128)S(1)} custom-call(f32[1]{0:T(128)} %bitcast.5.temp, f32[16,16,256]{2,1,0:T(8,128)S(1)} %score.1.best, bf16[4096,128]{1,0:T(8,128)(2,1)S(1)} %get-tuple-element.15.seg), custom_call_target="tpu_custom_call" | custom-call | tf_op jit(solution)/shard_map/gather/pallas_call | solution.py:414
  49.9 0.7 %loss.1 = (f32[1,16]{1,0:T(1,128)}, f32[1,1]{1,0:T(1,128)}) custom-call(f32[128,128]{1,0:T(8,128)S(1)} %gather.1.scores), custom_call_target="tpu_custom_call" | custom-call | tf_op jit(solution)/shard_map/loss/pallas_call | solution.py:424
Async XLA Ops:
  17.6 0.6 %copy-start = (s32[8,256]{1,0:T(8,128)}, s32[8,256]{1,0:T(8,128)S(1)}, u32[]{:S(2)}) copy-start(s32[8,256]{1,0:T(8,128)S(1)} %get-tuple-element.10.table) | copy-start | bytes 24580

commit v7 on v6

--- a/solution.py
+++ b/solution.py
@@ -14,7 +14,7 @@
 LANES = 8
 RING = 4
 HEAD = 320
-GROUP = 16
+GROUP = 8
 
 
 def iota(shape, dim):
@@ -57,6 +57,8 @@
     def doc_copy(j, slot):
         return pltpu.make_async_copy(d_hbm.at[pl.ds(j * dlen, HEAD)], d_buf.at[slot], d_sem.at[slot])
 
+    for j in range(2):
+        doc_copy(j, j).start()
     barrier = pltpu.get_barrier_semaphore()
     for rel in range(1, 8):
         pl.semaphore_signal(barrier, inc=1, device_id=place(rel)[0], device_id_type=MESH)
@@ -96,7 +98,7 @@
 
     for rel in (2, 4, 6, 1):
         send(0, rel)
-    for j in range(RING):
+    for j in range(2, RING):
         doc_copy(j, j).start()
 
     ins[1].wait()
@@ -107,26 +109,26 @@
     count = jnp.floor((last + (UNIT - 1.0)) * (1.0 / UNIT))
     sums = as_bf(iota((nd, nd), 0) >= iota((nd, nd), 1))
 
-    def listing(at, count, per, first):
+    def listing(at, count, first):
         upto = dot(sums, jnp.broadcast_to(count, (nd, 128)).astype(BF16))[:, 0:1]
         total = jnp.max(upto, axis=0, keepdims=True)
         slot_id = jnp.minimum(iota((nd, 256), 1).astype(F32), jnp.maximum(total - 1.0, 0.0))
         passed = slot_id >= upto
-        unit = slot_id[0:1] + first + jnp.sum(jnp.where(passed, per - count, 0.0), axis=0, keepdims=True)
+        unit = slot_id[0:1] + first + jnp.sum(jnp.where(passed, per_doc - count, 0.0), axis=0, keepdims=True)
         doc = jnp.sum(jnp.where(passed, 1.0, 0.0), axis=0, keepdims=True)
         table[at:at + 1, :] = unit.astype(jnp.int32)
         table[at + 1:at + 2, :] = doc.astype(jnp.int32)
         table[at + 2:at + 3, :] = jnp.broadcast_to(total, (1, 256)).astype(jnp.int32)
 
-    head = float(HEAD // UNIT)
-    listing(0, jnp.minimum(count, head), head, 0.0)
-    listing(4, jnp.maximum(count - head, 0.0), float(dlen // UNIT), head)
+    head, per_doc = float(HEAD // UNIT), float(dlen // UNIT)
+    listing(0, jnp.minimum(count, head), 0.0)
+    listing(4, jnp.maximum(count - head, 0.0), head)
 
     def project(j, carry):
         slot = lax.rem(j, RING)
         doc_copy(j, slot).wait()
-        p_ext[pl.ds(j * HEAD, HEAD), 0:128] = unit_rows(dot(d_buf[slot], w_buf[...]))
-        p_ext[pl.ds(j * HEAD, HEAD), 128:256] = mask_features(j, nmt[0:HEAD, :])
+        p_ext[pl.ds(j * dlen, HEAD), 0:128] = unit_rows(dot(d_buf[slot], w_buf[...]))
+        p_ext[pl.ds(j * dlen, HEAD), 128:256] = mask_features(j, nmt[0:HEAD, :])
 
         @pl.when(j + RING < nd)
         def _():
@@ -171,7 +173,7 @@
         copy.wait_send()
 
 
-def score_body(nd, rows, tiles, per_doc, hidden, table, q_all, p_head, nmt, w, d_hbm, out, q_list, best, p_tail, d_buf,
+def score_body(nd, rows, tiles, per_doc, hidden, table, q_all, nmt, w, d_hbm, out, p_ext, q_list, best, d_buf,
                sem, accs):
     n_head, n_tail = table[2, 0], table[6, 0]
     n_group = (n_tail + (GROUP - 1)) // GROUP
@@ -207,7 +209,7 @@
     def finish(slot, tile):
         out[tile] = jnp.max(jnp.maximum(best[0][slot], best[1][slot]), axis=1)
 
-    def sweep(at, count, row_of, src, is_last):
+    def sweep(count, item, is_last):
         n_trip = (count + (2 * LANES - 1)) // (2 * LANES)
         todo = jnp.where(count > 0, n_tile, 0)
 
@@ -216,15 +218,15 @@
             top = value[0:8]
             for r in range(1, UNIT // 8):
                 top = jnp.maximum(top, value[8 * r:8 * r + 8])
-            doc = table[at + 1, jnp.maximum(trip, 0) * (2 * LANES) + 2 * k + unit]
+            doc = item(trip * (2 * LANES) + 2 * k + unit, 1)
             best[unit][slot, doc] = jnp.maximum(best[unit][slot, doc], top)
 
         def step(slot, trip, prev_slot, prev_trip, first):
             for k in range(LANES):
                 for unit in range(2):
                     drain(unit, k, prev_slot, prev_trip)
-                    row = row_of(trip * (2 * LANES) + 2 * k + unit) * UNIT
-                    lhs = src[pl.ds(pl.multiple_of(row, UNIT), UNIT), :]
+                    row = item(trip * (2 * LANES) + 2 * k + unit, 0) * UNIT
+                    lhs = p_ext[pl.ds(pl.multiple_of(row, UNIT), UNIT), :]
                     pltpu.matmul_acc_lhs(accs[unit][k], lhs, load_staged_rhs=0 if first and k == 0 else None)
 
         push(0)
@@ -255,7 +257,15 @@
         best[unit][0] = floor
         for k in range(LANES):
             pltpu.matmul_pop(accs[unit][k])
-    sweep(0, n_head, lambda i: table[0, i], p_head, False)
+    n_first = n_head // (2 * LANES) * (2 * LANES)
+    n_left = n_head - n_first
+    n_second = n_left + n_tail
+
+    def second(i, what):
+        i = jnp.maximum(jnp.minimum(i, n_second - 1), 0)
+        return jnp.where(i < n_left, table[what, n_first + i], table[4 + what, jnp.maximum(i - n_left, 0)])
+
+    sweep(n_first, lambda i, what: table[what, jnp.maximum(i, 0)], False)
 
     depth = hidden // 256
     blank = jnp.zeros((256, 128), BF16)
@@ -269,43 +279,40 @@
 
     def project(g, carry):
         pltpu.make_async_copy(d_hbm.at[pl.ds(0, GROUP * UNIT)], d_buf.at[g], sem.at[g]).wait()
-        for half in range(2):
-            for k in range(depth):
-                for q in range(4):
-                    for unit in range(2):
-                        at = (half * 8 + unit * 4 + q) * UNIT
-                        pltpu.matmul_acc_lhs(accs[unit][half * 4 + q],
-                                             d_buf[g, at:at + UNIT, k * 256:(k + 1) * 256],
-                                             load_staged_rhs=0 if q == 0 else None)
-                push_w((k + 1) % depth)
+        for k in range(depth):
             for q in range(4):
                 for unit in range(2):
-                    index = g * GROUP + half * 8 + unit * 4 + q
-                    value = pltpu.matmul_pop(accs[unit][half * 4 + q])[:, 0:128]
-                    dst = pl.ds(pl.multiple_of(index * UNIT, UNIT), UNIT)
-                    doc = table[5, index]
-                    off = nmt[pl.ds(pl.multiple_of((table[4, index] - doc * per_doc) * UNIT, UNIT), UNIT), :]
-                    p_tail[dst, 0:128] = unit_rows(value)
-                    p_tail[dst, 128:256] = mask_features(doc, off)
+                    at = (unit * 4 + q) * UNIT
+                    pltpu.matmul_acc_lhs(accs[unit][q], d_buf[g, at:at + UNIT, k * 256:(k + 1) * 256],
+                                         load_staged_rhs=0 if q == 0 else None)
+            push_w((k + 1) % depth)
+        for q in range(4):
+            for unit in range(2):
+                block, doc = table[4, g * GROUP + unit * 4 + q], table[5, g * GROUP + unit * 4 + q]
+                value = pltpu.matmul_pop(accs[unit][q])[:, 0:128]
+                dst = pl.ds(pl.multiple_of(block * UNIT, UNIT), UNIT)
+                off = nmt[pl.ds(pl.multiple_of((block - doc * per_doc) * UNIT, UNIT), UNIT), :]
+                p_ext[dst, 0:128] = unit_rows(value)
+                p_ext[dst, 128:256] = mask_features(doc, off)
         return carry
 
     lax.fori_loop(0, n_group, project, 0)
     unstage()
 
-    sweep(4, n_tail, lambda i: jnp.minimum(i, n_tail - 1), p_tail, True)
+    sweep(n_second, second, True)
 
     def finish_all(tile, carry):
         finish(tile + 1, tile)
         return carry
 
-    lax.fori_loop(jnp.where(n_tail > 0, n_tile - 1, 0), n_tile, finish_all, 0)
-
-
-def score_kernel(nd, rows, tiles, per_doc, hidden, table, q_all, p_head, nmt, w, d_hbm, out, q_list, best0, best1, p_tail,
+    lax.fori_loop(jnp.where(n_second > 0, n_tile - 1, 0), n_tile, finish_all, 0)
+
+
+def score_kernel(nd, rows, tiles, per_doc, hidden, table, q_all, p_in, nmt, w, d_hbm, out, p_ext, q_list, best0, best1,
                  d_buf, sem):
     def body(*accs):
-        score_body(nd, rows, tiles, per_doc, hidden, table, q_all, p_head, nmt, w, d_hbm, out, q_list, (best0, best1),
-                   p_tail, d_buf, sem, (accs[:LANES], accs[LANES:]))
+        score_body(nd, rows, tiles, per_doc, hidden, table, q_all, nmt, w, d_hbm, out, p_ext, q_list, (best0, best1),
+                   d_buf, sem, (accs[:LANES], accs[LANES:]))
 
     pl.run_scoped(body, *[pltpu.ACC(0)((UNIT, 256), F32)] * LANES, *[pltpu.ACC(1)((UNIT, 256), F32)] * LANES)
 
@@ -372,7 +379,7 @@
             functools.partial(project_kernel, nq, qlen, nd, dlen),
             out_shape=[
                 pltpu.VMEM((rows * 8, 128), BF16),
-                pltpu.VMEM((nd * HEAD, 256), BF16),
+                pltpu.VMEM((nd * dlen, 256), BF16),
                 pltpu.VMEM((8, 256), jnp.int32),
                 pltpu.VMEM((rows * 8, nq * 8), BF16),
                 pltpu.VMEM((dlen, 128), BF16),
@@ -394,20 +401,20 @@
 
         tail_rows = nd * (dlen - HEAD)
         groups = tail_rows // (GROUP * UNIT)
-        best = pl.pallas_call(
+        best, _ = pl.pallas_call(
             functools.partial(score_kernel, nd, rows, tiles, dlen // UNIT, hidden),
-            out_shape=pltpu.VMEM((tiles, nd, 256), F32),
+            out_shape=[pltpu.VMEM((tiles, nd, 256), F32), pltpu.VMEM((nd * dlen, 256), BF16)],
             in_specs=[SMEM, VMEM, VMEM, VMEM, VMEM, ANY],
-            out_specs=VMEM,
+            out_specs=[VMEM, VMEM],
+            input_output_aliases={2: 1},
             scratch_shapes=[
                 pltpu.VMEM((rows * 8 + 512, 128), F32),
                 pltpu.VMEM((tiles + 1, nd, 8, 256), F32),
                 pltpu.VMEM((tiles + 1, nd, 8, 256), F32),
-                pltpu.VMEM((tail_rows, 256), BF16),
                 pltpu.VMEM((groups, GROUP * UNIT, hidden), BF16),
                 DMA((groups,)),
             ],
-            compiler_params=pltpu.CompilerParams(vmem_limit_bytes=50 * 2**20),
+            compiler_params=pltpu.CompilerParams(vmem_limit_bytes=36 * 2**20),
             name='score',
         )(table, vmem(q_all), vmem(p_head), vmem(nmt), vmem(w_vmem), hbm(doc_hidden.reshape(nd * dlen, hidden)))
 

time: 49.7 us -> 58.3 us (1.17)
  Pallas kernels: 48.7 us -> 57.7 us
  local copies, waits for them, and re-layouts: 0.59 us -> 0 us
    pallas_call x1, Pallas kernels: 6.62 us -> 12.1 us  [local_step(): pl.pallas_call(functools.partial(gather_kernel, nd, tiles), out_shape=plt...]
    pallas_call x1, Pallas kernels: 24.4 us -> 28.4 us  [local_step(): pl.pallas_call(functools.partial(score_kernel, nd, rows, tiles, dlen // U...]
    unnamed x2 -> x0, local copies, waits for them, and re-layouts: 0.59 us -> none
where the time goes in v7:
time: 58.3 us; the launch traced here: 59 us
  Pallas kernels  57.7 us (99%)
  between operations  1.3 us (2%)
    pallas_call x1, Pallas kernels, local_step(): pl.pallas_call(functools.partial(score_kernel, nd, rows, tiles, dlen // U...  28.4 us
    pallas_call x1, Pallas kernels, local_step(): pl.pallas_call(functools.partial(project_kernel, nq, qlen, nd, dlen), out...  16.6 us
    pallas_call x1, Pallas kernels, local_step(): pl.pallas_call(functools.partial(gather_kernel, nd, tiles), out_shape=plt...  12.1 us

profile of v7, /device:TPU:0, one launch (start us, length us, event | category | flops | bytes accessed | tf_op | source)
XLA Modules:
  0.0 59.0 jit_solution(9556223736062700970)
XLA Ops:
  0.6 16.6 %project.1 = (bf16[4096,128]{1,0:T(8,128)(2,1)S(1)}, bf16[12288,256]{1,0:T(8,128)(2,1)S(1)}, s32[8,256]{1,0:T(8,128)S(1)}, bf16[4096,128]{1,0:T(8,128)(2,1)S(1)}...) custom-call(bf16[512,1536]{1,0:T(8,128)(2,1)} %bitcast.8, bf16[12288,1536]{1,0:T(8,128)(2,1)} %bitcast.6, ...), custom_call_target="tpu_custom_call" | custom-call | tf_op jit(solution)/shard_map/project/pallas_call | solution.py:378
  17.2 28.4 %score.1 = (f32[16,16,256]{2,1,0:T(8,128)S(1)}, bf16[12288,256]{1,0:T(8,128)(2,1)S(1)}) custom-call(s32[8,256]{1,0:T(8,128)S(1)} %get-tuple-element.11.table, bf16[4096,128]{1,0:T(8,128)(2,1)S(1)} %get-tuple-element.12.q_all, bf16[12288,256]{1,0:T(8,128)(2,1)S(1)} %get-tuple-element.13.p_in, ...), custom_call_target="tpu_custom_call", output_to_operand_aliasing={{1}: (2, {})} | custom-call | tf_op jit(solution)/shard_map/score/pallas_call | solution.py:404
  46.2 12.1 %gather.1.scores = f32[128,128]{1,0:T(8,128)S(1)} custom-call(f32[1]{0:T(128)} %bitcast.5.temp, f32[16,16,256]{2,1,0:T(8,128)S(1)} %get-tuple-element.16.best, bf16[4096,128]{1,0:T(8,128)(2,1)S(1)} %get-tuple-element.17.seg), custom_call_target="tpu_custom_call" | custom-call | tf_op jit(solution)/shard_map/gather/pallas_call | solution.py:421
  58.4 0.7 %loss.1 = (f32[1,16]{1,0:T(1,128)}, f32[1,1]{1,0:T(1,128)}) custom-call(f32[128,128]{1,0:T(8,128)S(1)} %gather.1.scores), custom_call_target="tpu_custom_call" | custom-call | tf_op jit(solution)/shard_map/loss/pallas_call | solution.py:431
